TPU v7x, 32 devices: a whole 2x2x4 slice. The times are simulated.
32 devices in a mesh: grp: 8 (over z, x), sub: 4 (over y, core).
Axes of the slice: x: 2, y: 2, z: 4, core: 2. Of those that a mesh axis runs over, the one named last changes fastest.
Arguments:
- resid: bfloat16 [8, 4, 512, 512], P('grp', 'sub'), may hold values from -6 to 6
- neighbour_map: int32 [8, 4, 4], P('grp', 'sub'), may hold values from 0 to 3
- schur: bfloat16 [8, 4, 512, 512], P('grp', 'sub'), may hold values from -0.25 to 0.25
- deflation: bfloat16 [8, 4, 32, 512], P('grp', 'sub'), may hold values from -0.25 to 0.25
- forward_panels: bfloat16 [8, 128, 128], P('grp'), may hold values from -1 to 1
- block_inverses: bfloat16 [8, 128, 128], P('grp'), may hold values from -0.5 to 0.5
- scaling: float32 [8, 4, 512], P('grp', 'sub'), may hold values from 0.25 to 1
Outputs:
- applied: bfloat16 [8, 4, 512, 512], P('grp', 'sub')
All inputs are finite; a program needn't handle non-finite values.
Results may differ from a plain program's by a relative error of at most 0.013.
Values may be sent and summed in bfloat16 or wider, within the bound.
No kernel may reach another device: no remote copies, remote signals or barrier semaphores. Data moves between devices by JAX's collectives and lax.ppermute only.
A program may use at most 64 MiB of HBM per device.

v0:
```python
import jax
import jax.numpy as jnp
from jax import lax
from jax.sharding import PartitionSpec as P


def passed_along(block, axis, distance):
    devices = range(lax.axis_size(axis))
    route = [((i - distance) % len(devices), i) for i in devices]
    return lax.ppermute(block, axis, route)


def from_behind(block, axis, distance):
    devices = range(lax.axis_size(axis))
    route = [(i - distance, i) for i in devices if i - distance in devices]
    return lax.ppermute(block, axis, route)


def product(left, right):
    return jnp.dot(left, right, precision=lax.Precision.HIGHEST)


def assemble(field, neighbour_map):
    width = field.shape[-1] // neighbour_map.shape[-1]
    columns = jnp.repeat(neighbour_map[0, 0], width)[None, None, None, :]
    before_group = passed_along(field, "grp", 1)
    after_group = passed_along(field, "grp", -1)
    before_member = passed_along(field, "sub", 1)
    after_member = passed_along(field, "sub", -1)
    total = field.astype(jnp.float32)
    moved_all = (before_group, after_group, before_member, after_member)
    for code in range(4):
        total = total + jnp.where(
            columns == code, moved_all[code].astype(jnp.float32), jnp.float32(0.0)
        )
    return total


def body(resid, neighbour_map, schur, deflation, forward_panels, block_inverses, scaling):
    shared = assemble(resid, neighbour_map).astype(jnp.bfloat16)
    local_rows = shared[0, 0]
    local_schur = schur[0, 0]
    restricted = lax.dot_general(
        local_rows, deflation[0, 0], (((1,), (1,)), ((), ())), preferred_element_type=jnp.float32
    )
    before = jnp.dot(local_rows, local_schur, preferred_element_type=jnp.float32)
    coarse = lax.all_to_all(
        restricted.astype(jnp.bfloat16), "sub", split_axis=0, concat_axis=1, tiled=True
    ).astype(restricted.dtype)
    panel = forward_panels[0].astype(jnp.float32)

    def advance(step, state):
        received = from_behind(state, "grp", 1)
        return coarse + product(received, panel)

    carried = lax.fori_loop(0, lax.axis_size("grp") - 1, advance, coarse)
    solved = product(carried, block_inverses[0].astype(jnp.float32))
    lifted = lax.all_to_all(
        solved.astype(jnp.bfloat16), "sub", split_axis=1, concat_axis=0, tiled=True
    ).astype(solved.dtype)
    correction = product(lifted, deflation[0, 0].astype(jnp.float32))
    correction_low = correction.astype(jnp.bfloat16)
    after = jnp.dot(correction_low, local_schur, preferred_element_type=jnp.float32)
    local = (correction + scaling[0, 0][None, :] * (before - after)).astype(jnp.bfloat16)
    return assemble(local[None, None], neighbour_map).astype(jnp.bfloat16)


def solution(mesh):
    return jax.shard_map(
        body,
        mesh=mesh,
        in_specs=(
            P("grp", "sub", None, None),
            P("grp", "sub", None),
            P("grp", "sub", None, None),
            P("grp", "sub", None, None),
            P("grp", None, None),
            P("grp", None, None),
            P("grp", "sub", None),
        ),
        out_specs=P("grp", "sub", None, None),
        check_vma=False,
    )
```

profile of v0, /device:TPU:0, one launch (start us, length us, event | category | flops | bytes accessed | tf_op | source)
XLA Modules:
  0.0 124.5 jit_solution(6189228506094857152)
XLA Ops:
  0.0 3.0 %collective-permute-start.1 = (bf16[1,1,512,512]{3,2,1,0:T(8,128)(2,1)}, bf16[1,1,512,512]{3,2,1,0:T(8,128)(2,1)S(1)}, u32[]{:S(2)}, u32[]{:S(2)}) collective-permute-start(bf16[1,1,512,512]{3,2,1,0:T(8,128)(2,1)} %param.9), channel_id=1, source_target_pairs={{28,0},{0,4},{4,8},{8,12},{12,16},{16,20},{20,24},{24,28},{29,1},{... | collective-permute-start | bytes 1572872 | tf_op jit(solution)/shard_map/ppermute | solution.py:10
  3.0 3.1 %collective-permute-start.2 = (bf16[1,1,512,512]{3,2,1,0:T(8,128)(2,1)}, bf16[1,1,512,512]{3,2,1,0:T(8,128)(2,1)S(1)}, u32[]{:S(2)}, u32[]{:S(2)}) collective-permute-start(bf16[1,1,512,512]{3,2,1,0:T(8,128)(2,1)} %param.9), channel_id=1, source_target_pairs={{4,0},{8,4},{12,8},{16,12},{20,16},{24,20},{28,24},{0,28},{5,1},{9... | collective-permute-start | bytes 1572872 | tf_op jit(solution)/shard_map/ppermute | solution.py:10
  8.6 17.1 %collective-permute-done.1 = bf16[1,1,512,512]{3,2,1,0:T(8,128)(2,1)S(1)} collective-permute-done((bf16[1,1,512,512]{3,2,1,0:T(8,128)(2,1)}, bf16[1,1,512,512]{3,2,1,0:T(8,128)(2,1)S(1)}, u32[]{:S(2)}, u32[]{:S(2)}) %collective-permute-start.1) | collective-permute-done | bytes 524320 | tf_op jit(solution)/shard_map/ppermute | solution.py:10
  25.7 2.1 %collective-permute-done.2 = bf16[1,1,512,512]{3,2,1,0:T(8,128)(2,1)S(1)} collective-permute-done((bf16[1,1,512,512]{3,2,1,0:T(8,128)(2,1)}, bf16[1,1,512,512]{3,2,1,0:T(8,128)(2,1)S(1)}, u32[]{:S(2)}, u32[]{:S(2)}) %collective-permute-start.2) | collective-permute-done | bytes 524320 | tf_op jit(solution)/shard_map/ppermute | solution.py:10
  30.2 3.4 %all-to-all-start = ((bf16[4,128,32]{1,2,0:T(8,128)(2,1)}), bf16[4,128,32]{1,2,0:T(8,128)(2,1)S(1)}, u32[]{:S(2)}, u32[]{:S(2)}) async-start(bf16[4,128,32]{1,2,0:T(8,128)(2,1)} %bitcast.58), calls=%async_computation | async-start | bytes 65536 | tf_op jit(solution)/shard_map/all_to_all | solution.py:47
  33.7 3.9 %all-to-all-done = bf16[4,128,32]{1,2,0:T(8,128)(2,1)S(1)} async-done(((bf16[4,128,32]{1,2,0:T(8,128)(2,1)}), bf16[4,128,32]{1,2,0:T(8,128)(2,1)S(1)}, u32[]{:S(2)}, u32[]{:S(2)}) %all-to-all-start) | async-done | bytes 32800 | tf_op jit(solution)/shard_map/all_to_all | solution.py:47
  37.7 47.6 %while.10 = (s32[]{:T(128)}, f32[128,128]{1,0:T(8,128)S(1)}, f32[128,128]{1,0:T(8,128)S(1)}, f32[128,128]{1,0:T(8,128)S(1)}, s32[]{:T(128)}) while((s32[]{:T(128)}, f32[128,128]{1,0:T(8,128)S(1)}, f32[128,128]{1,0:T(8,128)S(1)}, f32[128,128]{1,0:T(8,128)S(1)}, s32[]{:T(128)}) %tuple.25), condition=%wide.region_1.2_spmd, body=%wide.region_0.1_spmd.sunk | while | flops 25182208 | bytes 524389 | solution.py:56
  37.7 2.2 %collective-permute-start = (f32[128,128]{1,0:T(8,128)S(1)}, f32[128,128]{1,0:T(8,128)S(1)}, u32[]{:S(2)}, u32[]{:S(2)}) collective-permute-start(f32[128,128]{1,0:T(8,128)S(1)} %get-tuple-element.83), channel_id=1, source_target_pairs={{0,4},{4,8},{8,12},{12,16},{16,20},{20,24},{24,28},{1,5},{5,9},{9,... | collective-permute-start | bytes 196616 | tf_op jit(solution)/shard_map/while/body/eval_jaxpr/ppermute | solution.py:16
  39.9 1.9 %collective-permute-done = f32[128,128]{1,0:T(8,128)S(1)} collective-permute-done((f32[128,128]{1,0:T(8,128)S(1)}, f32[128,128]{1,0:T(8,128)S(1)}, u32[]{:S(2)}, u32[]{:S(2)}) %collective-permute-start) | collective-permute-done | bytes 65568 | tf_op jit(solution)/shard_map/while/body/eval_jaxpr/ppermute | solution.py:16
  42.0 4.3 %collective-permute-start = (f32[128,128]{1,0:T(8,128)S(1)}, f32[128,128]{1,0:T(8,128)S(1)}, u32[]{:S(2)}, u32[]{:S(2)}) collective-permute-start(f32[128,128]{1,0:T(8,128)S(1)} %get-tuple-element.83), channel_id=1, source_target_pairs={{0,4},{4,8},{8,12},{12,16},{16,20},{20,24},{24,28},{1,5},{5,9},{9,... | collective-permute-start | bytes 196616 | tf_op jit(solution)/shard_map/while/body/eval_jaxpr/ppermute | solution.py:16
  46.4 1.9 %collective-permute-done = f32[128,128]{1,0:T(8,128)S(1)} collective-permute-done((f32[128,128]{1,0:T(8,128)S(1)}, f32[128,128]{1,0:T(8,128)S(1)}, u32[]{:S(2)}, u32[]{:S(2)}) %collective-permute-start) | collective-permute-done | bytes 65568 | tf_op jit(solution)/shard_map/while/body/eval_jaxpr/ppermute | solution.py:16
  48.5 5.2 %collective-permute-start = (f32[128,128]{1,0:T(8,128)S(1)}, f32[128,128]{1,0:T(8,128)S(1)}, u32[]{:S(2)}, u32[]{:S(2)}) collective-permute-start(f32[128,128]{1,0:T(8,128)S(1)} %get-tuple-element.83), channel_id=1, source_target_pairs={{0,4},{4,8},{8,12},{12,16},{16,20},{20,24},{24,28},{1,5},{5,9},{9,... | collective-permute-start | bytes 196616 | tf_op jit(solution)/shard_map/while/body/eval_jaxpr/ppermute | solution.py:16
  53.6 1.9 %collective-permute-done = f32[128,128]{1,0:T(8,128)S(1)} collective-permute-done((f32[128,128]{1,0:T(8,128)S(1)}, f32[128,128]{1,0:T(8,128)S(1)}, u32[]{:S(2)}, u32[]{:S(2)}) %collective-permute-start) | collective-permute-done | bytes 65568 | tf_op jit(solution)/shard_map/while/body/eval_jaxpr/ppermute | solution.py:16
  55.8 5.2 %collective-permute-start = (f32[128,128]{1,0:T(8,128)S(1)}, f32[128,128]{1,0:T(8,128)S(1)}, u32[]{:S(2)}, u32[]{:S(2)}) collective-permute-start(f32[128,128]{1,0:T(8,128)S(1)} %get-tuple-element.83), channel_id=1, source_target_pairs={{0,4},{4,8},{8,12},{12,16},{16,20},{20,24},{24,28},{1,5},{5,9},{9,... | collective-permute-start | bytes 196616 | tf_op jit(solution)/shard_map/while/body/eval_jaxpr/ppermute | solution.py:16
  63.0 5.2 %collective-permute-start = (f32[128,128]{1,0:T(8,128)S(1)}, f32[128,128]{1,0:T(8,128)S(1)}, u32[]{:S(2)}, u32[]{:S(2)}) collective-permute-start(f32[128,128]{1,0:T(8,128)S(1)} %get-tuple-element.83), channel_id=1, source_target_pairs={{0,4},{4,8},{8,12},{12,16},{16,20},{20,24},{24,28},{1,5},{5,9},{9,... | collective-permute-start | bytes 196616 | tf_op jit(solution)/shard_map/while/body/eval_jaxpr/ppermute | solution.py:16
  70.3 5.4 %collective-permute-start = (f32[128,128]{1,0:T(8,128)S(1)}, f32[128,128]{1,0:T(8,128)S(1)}, u32[]{:S(2)}, u32[]{:S(2)}) collective-permute-start(f32[128,128]{1,0:T(8,128)S(1)} %get-tuple-element.83), channel_id=1, source_target_pairs={{0,4},{4,8},{8,12},{12,16},{16,20},{20,24},{24,28},{1,5},{5,9},{9,... | collective-permute-start | bytes 196616 | tf_op jit(solution)/shard_map/while/body/eval_jaxpr/ppermute | solution.py:16
  75.8 1.9 %collective-permute-done = f32[128,128]{1,0:T(8,128)S(1)} collective-permute-done((f32[128,128]{1,0:T(8,128)S(1)}, f32[128,128]{1,0:T(8,128)S(1)}, u32[]{:S(2)}, u32[]{:S(2)}) %collective-permute-start) | collective-permute-done | bytes 65568 | tf_op jit(solution)/shard_map/while/body/eval_jaxpr/ppermute | solution.py:16
  77.9 5.3 %collective-permute-start = (f32[128,128]{1,0:T(8,128)S(1)}, f32[128,128]{1,0:T(8,128)S(1)}, u32[]{:S(2)}, u32[]{:S(2)}) collective-permute-start(f32[128,128]{1,0:T(8,128)S(1)} %get-tuple-element.83), channel_id=1, source_target_pairs={{0,4},{4,8},{8,12},{12,16},{16,20},{20,24},{24,28},{1,5},{5,9},{9,... | collective-permute-start | bytes 196616 | tf_op jit(solution)/shard_map/while/body/eval_jaxpr/ppermute | solution.py:16
  86.2 3.3 %all-to-all-start.1 = ((bf16[128,4,32]{0,2,1:T(8,128)(2,1)}), bf16[128,4,32]{0,2,1:T(8,128)(2,1)S(1)}, u32[]{:S(2)}, u32[]{:S(2)}) async-start(bf16[128,4,32]{0,2,1:T(8,128)(2,1)} %bitcast.15), calls=%async_computation.1 | async-start | bytes 65536 | tf_op jit(solution)/shard_map/all_to_all | solution.py:58
  89.9 3.5 %all-to-all-done.1 = bf16[128,4,32]{0,2,1:T(8,128)(2,1)S(1)} async-done(((bf16[128,4,32]{0,2,1:T(8,128)(2,1)}), bf16[128,4,32]{0,2,1:T(8,128)(2,1)S(1)}, u32[]{:S(2)}, u32[]{:S(2)}) %all-to-all-start.1) | async-done | bytes 32800 | tf_op jit(solution)/shard_map/all_to_all | solution.py:58
  94.5 3.3 %collective-permute-start.5 = (bf16[1,1,512,512]{3,2,1,0:T(8,128)(2,1)S(1)}, bf16[1,1,512,512]{3,2,1,0:T(8,128)(2,1)S(1)}, u32[]{:S(2)}, u32[]{:S(2)}) collective-permute-start(bf16[1,1,512,512]{3,2,1,0:T(8,128)(2,1)S(1)} %fusion.3), channel_id=1, source_target_pairs={{28,0},{0,4},{4,8},{8,12},{12,16},{16,20},{20,24},{24,28},{29,1},{... | collective-permute-start | bytes 1572872 | tf_op jit(solution)/shard_map/ppermute | solution.py:10
  97.8 2.4 %collective-permute-start.6 = (bf16[1,1,512,512]{3,2,1,0:T(8,128)(2,1)S(1)}, bf16[1,1,512,512]{3,2,1,0:T(8,128)(2,1)S(1)}, u32[]{:S(2)}, u32[]{:S(2)}) collective-permute-start(bf16[1,1,512,512]{3,2,1,0:T(8,128)(2,1)S(1)} %fusion.3), channel_id=1, source_target_pairs={{4,0},{8,4},{12,8},{16,12},{20,16},{24,20},{28,24},{0,28},{5,1},{9... | collective-permute-start | bytes 1572872 | tf_op jit(solution)/shard_map/ppermute | solution.py:10
  102.0 18.1 %collective-permute-done.5 = bf16[1,1,512,512]{3,2,1,0:T(8,128)(2,1)S(1)} collective-permute-done((bf16[1,1,512,512]{3,2,1,0:T(8,128)(2,1)S(1)}, bf16[1,1,512,512]{3,2,1,0:T(8,128)(2,1)S(1)}, u32[]{:S(2)}, u32[]{:S(2)}) %collective-permute-start.5) | collective-permute-done | bytes 524320 | tf_op jit(solution)/shard_map/ppermute | solution.py:10
  120.1 3.1 %collective-permute-done.6 = bf16[1,1,512,512]{3,2,1,0:T(8,128)(2,1)S(1)} collective-permute-done((bf16[1,1,512,512]{3,2,1,0:T(8,128)(2,1)S(1)}, bf16[1,1,512,512]{3,2,1,0:T(8,128)(2,1)S(1)}, u32[]{:S(2)}, u32[]{:S(2)}) %collective-permute-start.6) | collective-permute-done | bytes 524320 | tf_op jit(solution)/shard_map/ppermute | solution.py:10
  (43 shorter events, 17.6 us)
Async XLA Ops:
  0.0 89.4 %copy-start = (bf16[1,1,512,512]{3,2,1,0:T(8,128)(2,1)S(1)}, bf16[1,1,512,512]{3,2,1,0:T(8,128)(2,1)}, u32[]{:S(2)}) copy-start(bf16[1,1,512,512]{3,2,1,0:T(8,128)(2,1)} %param.11) | copy-start | bytes 1572868
  0.0 25.7 %collective-permute-start.1 = (bf16[1,1,512,512]{3,2,1,0:T(8,128)(2,1)}, bf16[1,1,512,512]{3,2,1,0:T(8,128)(2,1)S(1)}, u32[]{:S(2)}, u32[]{:S(2)}) collective-permute-start(bf16[1,1,512,512]{3,2,1,0:T(8,128)(2,1)} %param.9), channel_id=1, source_target_pairs={{28,0},{0,4},{4,8},{8,12},{12,16},{16,20},{20,24},{24,28},{29,1},{... | collective-permute-start | bytes 1572872 | tf_op jit(solution)/shard_map/ppermute | solution.py:10
  3.0 24.8 %collective-permute-start.2 = (bf16[1,1,512,512]{3,2,1,0:T(8,128)(2,1)}, bf16[1,1,512,512]{3,2,1,0:T(8,128)(2,1)S(1)}, u32[]{:S(2)}, u32[]{:S(2)}) collective-permute-start(bf16[1,1,512,512]{3,2,1,0:T(8,128)(2,1)} %param.9), channel_id=1, source_target_pairs={{4,0},{8,4},{12,8},{16,12},{20,16},{24,20},{28,24},{0,28},{5,1},{9... | collective-permute-start | bytes 1572872 | tf_op jit(solution)/shard_map/ppermute | solution.py:10
  6.1 21.7 %collective-permute-start.3 = (bf16[1,1,512,512]{3,2,1,0:T(8,128)(2,1)}, bf16[1,1,512,512]{3,2,1,0:T(8,128)(2,1)S(1)}, u32[]{:S(2)}, u32[]{:S(2)}) collective-permute-start(bf16[1,1,512,512]{3,2,1,0:T(8,128)(2,1)} %param.9), channel_id=1, source_target_pairs={{3,0},{0,1},{1,2},{2,3},{7,4},{4,5},{5,6},{6,7},{11,8},{8,9},{9,10... | collective-permute-start | bytes 1572872 | tf_op jit(solution)/shard_map/ppermute | solution.py:10
  6.1 21.7 %collective-permute-start.4 = (bf16[1,1,512,512]{3,2,1,0:T(8,128)(2,1)}, bf16[1,1,512,512]{3,2,1,0:T(8,128)(2,1)S(1)}, u32[]{:S(2)}, u32[]{:S(2)}) collective-permute-start(bf16[1,1,512,512]{3,2,1,0:T(8,128)(2,1)} %param.9), channel_id=1, source_target_pairs={{1,0},{2,1},{3,2},{0,3},{5,4},{6,5},{7,6},{4,7},{9,8},{10,9},{11,1... | collective-permute-start | bytes 1572872 | tf_op jit(solution)/shard_map/ppermute | solution.py:10
  27.8 1.5 %copy-start.1 = (bf16[1,1,32,512]{3,2,1,0:T(8,128)(2,1)S(1)}, bf16[1,1,32,512]{3,2,1,0:T(8,128)(2,1)}, u32[]{:S(2)}) copy-start(bf16[1,1,32,512]{3,2,1,0:T(8,128)(2,1)} %param.12) | copy-start | bytes 98308
  30.2 3.4 %copy-start.2 = (bf16[1,128,128]{2,1,0:T(8,128)(2,1)S(1)}, bf16[1,128,128]{2,1,0:T(8,128)(2,1)}, u32[]{:S(2)}) copy-start(bf16[1,128,128]{2,1,0:T(8,128)(2,1)} %param.13) | copy-start | bytes 98308
  30.2 7.3 %all-to-all-start = ((bf16[4,128,32]{1,2,0:T(8,128)(2,1)}), bf16[4,128,32]{1,2,0:T(8,128)(2,1)S(1)}, u32[]{:S(2)}, u32[]{:S(2)}) async-start(bf16[4,128,32]{1,2,0:T(8,128)(2,1)} %bitcast.58), calls=%async_computation | async-start | bytes 65536 | tf_op jit(solution)/shard_map/all_to_all | solution.py:47
  37.7 47.6 %copy-start.3 = (bf16[1,128,128]{2,1,0:T(8,128)(2,1)S(1)}, bf16[1,128,128]{2,1,0:T(8,128)(2,1)}, u32[]{:S(2)}) copy-start(bf16[1,128,128]{2,1,0:T(8,128)(2,1)} %param.14) | copy-start | bytes 98308
  37.7 4.1 %collective-permute-start = (f32[128,128]{1,0:T(8,128)S(1)}, f32[128,128]{1,0:T(8,128)S(1)}, u32[]{:S(2)}, u32[]{:S(2)}) collective-permute-start(f32[128,128]{1,0:T(8,128)S(1)} %get-tuple-element.83), channel_id=1, source_target_pairs={{0,4},{4,8},{8,12},{12,16},{16,20},{20,24},{24,28},{1,5},{5,9},{9,... | collective-permute-start | bytes 196616 | tf_op jit(solution)/shard_map/while/body/eval_jaxpr/ppermute | solution.py:16
  42.0 6.2 %collective-permute-start = (f32[128,128]{1,0:T(8,128)S(1)}, f32[128,128]{1,0:T(8,128)S(1)}, u32[]{:S(2)}, u32[]{:S(2)}) collective-permute-start(f32[128,128]{1,0:T(8,128)S(1)} %get-tuple-element.83), channel_id=1, source_target_pairs={{0,4},{4,8},{8,12},{12,16},{16,20},{20,24},{24,28},{1,5},{5,9},{9,... | collective-permute-start | bytes 196616 | tf_op jit(solution)/shard_map/while/body/eval_jaxpr/ppermute | solution.py:16
  48.5 7.1 %collective-permute-start = (f32[128,128]{1,0:T(8,128)S(1)}, f32[128,128]{1,0:T(8,128)S(1)}, u32[]{:S(2)}, u32[]{:S(2)}) collective-permute-start(f32[128,128]{1,0:T(8,128)S(1)} %get-tuple-element.83), channel_id=1, source_target_pairs={{0,4},{4,8},{8,12},{12,16},{16,20},{20,24},{24,28},{1,5},{5,9},{9,... | collective-permute-start | bytes 196616 | tf_op jit(solution)/shard_map/while/body/eval_jaxpr/ppermute | solution.py:16
  55.8 7.1 %collective-permute-start = (f32[128,128]{1,0:T(8,128)S(1)}, f32[128,128]{1,0:T(8,128)S(1)}, u32[]{:S(2)}, u32[]{:S(2)}) collective-permute-start(f32[128,128]{1,0:T(8,128)S(1)} %get-tuple-element.83), channel_id=1, source_target_pairs={{0,4},{4,8},{8,12},{12,16},{16,20},{20,24},{24,28},{1,5},{5,9},{9,... | collective-permute-start | bytes 196616 | tf_op jit(solution)/shard_map/while/body/eval_jaxpr/ppermute | solution.py:16
  63.0 7.1 %collective-permute-start = (f32[128,128]{1,0:T(8,128)S(1)}, f32[128,128]{1,0:T(8,128)S(1)}, u32[]{:S(2)}, u32[]{:S(2)}) collective-permute-start(f32[128,128]{1,0:T(8,128)S(1)} %get-tuple-element.83), channel_id=1, source_target_pairs={{0,4},{4,8},{8,12},{12,16},{16,20},{20,24},{24,28},{1,5},{5,9},{9,... | collective-permute-start | bytes 196616 | tf_op jit(solution)/shard_map/while/body/eval_jaxpr/ppermute | solution.py:16
  70.3 7.4 %collective-permute-start = (f32[128,128]{1,0:T(8,128)S(1)}, f32[128,128]{1,0:T(8,128)S(1)}, u32[]{:S(2)}, u32[]{:S(2)}) collective-permute-start(f32[128,128]{1,0:T(8,128)S(1)} %get-tuple-element.83), channel_id=1, source_target_pairs={{0,4},{4,8},{8,12},{12,16},{16,20},{20,24},{24,28},{1,5},{5,9},{9,... | collective-permute-start | bytes 196616 | tf_op jit(solution)/shard_map/while/body/eval_jaxpr/ppermute | solution.py:16
  77.9 7.2 %collective-permute-start = (f32[128,128]{1,0:T(8,128)S(1)}, f32[128,128]{1,0:T(8,128)S(1)}, u32[]{:S(2)}, u32[]{:S(2)}) collective-permute-start(f32[128,128]{1,0:T(8,128)S(1)} %get-tuple-element.83), channel_id=1, source_target_pairs={{0,4},{4,8},{8,12},{12,16},{16,20},{20,24},{24,28},{1,5},{5,9},{9,... | collective-permute-start | bytes 196616 | tf_op jit(solution)/shard_map/while/body/eval_jaxpr/ppermute | solution.py:16
  86.2 7.2 %all-to-all-start.1 = ((bf16[128,4,32]{0,2,1:T(8,128)(2,1)}), bf16[128,4,32]{0,2,1:T(8,128)(2,1)S(1)}, u32[]{:S(2)}, u32[]{:S(2)}) async-start(bf16[128,4,32]{0,2,1:T(8,128)(2,1)} %bitcast.15), calls=%async_computation.1 | async-start | bytes 65536 | tf_op jit(solution)/shard_map/all_to_all | solution.py:58
  93.3 0.7 copy-start.4
  94.5 25.6 %collective-permute-start.5 = (bf16[1,1,512,512]{3,2,1,0:T(8,128)(2,1)S(1)}, bf16[1,1,512,512]{3,2,1,0:T(8,128)(2,1)S(1)}, u32[]{:S(2)}, u32[]{:S(2)}) collective-permute-start(bf16[1,1,512,512]{3,2,1,0:T(8,128)(2,1)S(1)} %fusion.3), channel_id=1, source_target_pairs={{28,0},{0,4},{4,8},{8,12},{12,16},{16,20},{20,24},{24,28},{29,1},{... | collective-permute-start | bytes 1572872 | tf_op jit(solution)/shard_map/ppermute | solution.py:10
  97.8 25.4 %collective-permute-start.6 = (bf16[1,1,512,512]{3,2,1,0:T(8,128)(2,1)S(1)}, bf16[1,1,512,512]{3,2,1,0:T(8,128)(2,1)S(1)}, u32[]{:S(2)}, u32[]{:S(2)}) collective-permute-start(bf16[1,1,512,512]{3,2,1,0:T(8,128)(2,1)S(1)} %fusion.3), channel_id=1, source_target_pairs={{4,0},{8,4},{12,8},{16,12},{20,16},{24,20},{28,24},{0,28},{5,1},{9... | collective-permute-start | bytes 1572872 | tf_op jit(solution)/shard_map/ppermute | solution.py:10
  100.2 23.0 %collective-permute-start.7 = (bf16[1,1,512,512]{3,2,1,0:T(8,128)(2,1)S(1)}, bf16[1,1,512,512]{3,2,1,0:T(8,128)(2,1)S(1)}, u32[]{:S(2)}, u32[]{:S(2)}) collective-permute-start(bf16[1,1,512,512]{3,2,1,0:T(8,128)(2,1)S(1)} %fusion.3), channel_id=1, source_target_pairs={{3,0},{0,1},{1,2},{2,3},{7,4},{4,5},{5,6},{6,7},{11,8},{8,9},{9,10... | collective-permute-start | bytes 1572872 | tf_op jit(solution)/shard_map/ppermute | solution.py:10
  100.2 23.0 %collective-permute-start.8 = (bf16[1,1,512,512]{3,2,1,0:T(8,128)(2,1)S(1)}, bf16[1,1,512,512]{3,2,1,0:T(8,128)(2,1)S(1)}, u32[]{:S(2)}, u32[]{:S(2)}) collective-permute-start(bf16[1,1,512,512]{3,2,1,0:T(8,128)(2,1)S(1)} %fusion.3), channel_id=1, source_target_pairs={{1,0},{2,1},{3,2},{0,3},{5,4},{6,5},{7,6},{4,7},{9,8},{10,9},{11,1... | collective-permute-start | bytes 1572872 | tf_op jit(solution)/shard_map/ppermute | solution.py:10
where the time goes:
time: 125 us; the launch traced here: 124 us
  waiting for transfers between devices  61 us (49%)
  starting transfers between devices  54.7 us (44%)
  matrix products  3.7 us (3%)
  other arithmetic  3.46 us (3%)
  local copies, waits for them, and re-layouts  1.27 us (1%)
    ppermute x8, waiting for transfers between devices, passed_along(): return lax.ppermute(block, axis, route)  40.4 us
    ppermute x7, starting transfers between devices, from_behind(): return lax.ppermute(block, axis, route)  32.7 us
    ppermute x8, starting transfers between devices, passed_along(): return lax.ppermute(block, axis, route)  15.3 us
    ppermute x7, waiting for transfers between devices, from_behind(): return lax.ppermute(block, axis, route)  13.2 us
    all_to_all x1, waiting for transfers between devices, body(): lax.all_to_all(restricted.astype(jnp.bfloat16), 'sub', split_axis=0, conc...  3.89 us
    all_to_all x1, waiting for transfers between devices, body(): lax.all_to_all(solved.astype(jnp.bfloat16), 'sub', split_axis=1, concat_a...  3.46 us
    all_to_all x1, starting transfers between devices, body(): lax.all_to_all(restricted.astype(jnp.bfloat16), 'sub', split_axis=0, conc...  3.4 us
    all_to_all x1, starting transfers between devices, body(): lax.all_to_all(solved.astype(jnp.bfloat16), 'sub', split_axis=1, concat_a...  3.26 us
  transfers between devices with their start and end apart: 17, of which 13 were waited for; matrix products, arithmetic and copies ran while one was open for 1% of the time, Pallas kernels for 0%

commit v1 on v0

v1 whole, which is shorter than its diff:
```python
import functools

import jax
import jax.numpy as jnp
from jax import lax
from jax.experimental import pallas as pl
from jax.experimental.pallas import tpu as pltpu
from jax.sharding import PartitionSpec as P


MOST_WEIGHTS = 1 << 20
CUTS_ONE = (4,)
CUTS_TWO = (3,)
VMEM = pl.BlockSpec(memory_space=pltpu.VMEM)
SMEM = pl.BlockSpec(memory_space=pltpu.SMEM)


def swap(block, axis, partner):
    route = [(i, partner(i)) for i in range(lax.axis_size(axis))]
    return lax.ppermute(block, axis, route)


def near(i):
    return i ^ 1


def far(size):
    return lambda i: (i + 1) % size if i % 2 else (i - 1) % size


def onward(size):
    return lambda i: (i + 2) % size if i % 2 == 0 else (i - 2) % size


def chunk_sizes(rows, eighths):
    ends = [rows * eighth // 8 for eighth in (0, *eighths, 8)]
    return [high - low for low, high in zip(ends, ends[1:])]


def chosen(neighbour_map):
    codes = neighbour_map[0, 0]
    odd_g, odd_m = lax.axis_index("grp") % 2, lax.axis_index("sub") % 2
    return jnp.where(codes < 2, (codes + 1 + odd_g) % 2, 2 + (codes + 1 + odd_m) % 2)


def exact(left, right):
    return jnp.dot(left, right, precision=lax.Precision.HIGHEST)


def bits_of(groups):
    bits, bit = [], 2
    while bit < groups:
        bits.append(bit)
        bit *= 2
    return [*bits, 1]


def weights_kernel(groups, vectors, place, stack, other, weights, below, picked):
    here, member = place[0], place[1]
    kb = stack.shape[3]
    targets = [place[2 + i] for i in range(weights.shape[0] // kb)]
    even, upper = member % 2 == 0, member // 2 % 2 == 0

    def slot(h):
        offset = h ^ here
        return sum(((offset // bit) % 2) << k for k, bit in enumerate(bits_of(groups)))

    def block(h, mine):
        own, twin = (jnp.where(mine, stack[i, slot(h)], other[i, slot(h)]) for i in range(2))
        return jnp.concatenate([jnp.where(upper, own, twin), jnp.where(upper, twin, own)])

    below[...] = jnp.zeros_like(below)
    for h in range(groups - 1, -1, -1):
        if h < groups - 1:
            value = below[...]
            high = value.astype(jnp.bfloat16)
            low = (value - high.astype(jnp.float32)).astype(jnp.bfloat16)
            left = block(h + 1, even)
            below[...] = jnp.dot(left, high, preferred_element_type=jnp.float32) + jnp.dot(
                left, low, preferred_element_type=jnp.float32
            )
        for i, target in enumerate(targets):

            @pl.when(target == h)
            def _():
                below[:, i * kb : (i + 1) * kb] = block(h, ~even).astype(jnp.float32)

        mine = below[pl.ds(pl.multiple_of(member * vectors, vectors), vectors)]
        picked[pl.ds(pl.multiple_of(slot(h) * vectors, vectors), vectors)] = mine
    weights[...] = picked[...].T.astype(jnp.bfloat16)


def coarse_weights(forward_panels, block_inverses, targets, vectors):
    groups, here, member = lax.axis_size("grp"), lax.axis_index("grp"), lax.axis_index("sub")
    kb = forward_panels.shape[-1]
    half = kb // 2
    kind = jnp.where(member % 2 == 0, forward_panels[0], block_inverses[0])
    stack = jnp.where(member // 2 % 2 == 0, kind[:half], kind[half:])[None]
    for bit in bits_of(groups):
        stack = jnp.concatenate([stack, swap(stack, "grp", lambda i: i ^ bit)])
    stack = jnp.stack([stack, swap(stack, "sub", lambda i: i ^ 2)])
    other = swap(stack, "sub", near)
    rows = len(targets) * kb
    return call(
        functools.partial(weights_kernel, groups, vectors),
        jax.ShapeDtypeStruct((rows, groups * vectors), jnp.bfloat16),
        [SMEM, VMEM, VMEM],
        [pltpu.VMEM((kb, rows), jnp.float32), pltpu.VMEM((groups * vectors, rows), jnp.float32)],
        4 * groups * kb * kb * rows,
        jnp.stack([here, member, *targets]).astype(jnp.int32), stack, other,
    )


def join_kernel(blocks, counts, pick, own, defl, *refs):
    *pieces, shared, restricted = refs
    width = own.shape[1] // blocks
    fields = [[pieces.pop(0) for _ in range(count)] for count in counts]
    for n in range(blocks):
        cols = slice(n * width, (n + 1) * width)
        for code, field in enumerate(fields):

            @pl.when(pick[n] == code)
            def _():
                row = 0
                for ref in field:
                    place = slice(row, row + ref.shape[0])
                    total = own[place, cols].astype(jnp.float32) + ref[:, cols].astype(jnp.float32)
                    shared[place, cols] = total.astype(jnp.bfloat16)
                    row += ref.shape[0]

    restricted[0] = lax.dot_general(
        defl[...], shared[...], (((1,), (1,)), ((), ())), preferred_element_type=jnp.float32
    ).astype(jnp.bfloat16)


def basis_kernel(defl, schur, scale, basis):
    defl_schur = jnp.dot(defl[...], schur[...], preferred_element_type=jnp.float32)
    basis[...] = (defl[...].astype(jnp.float32) - scale[...] * defl_schur).astype(jnp.bfloat16)


def base_kernel(shared, basis, schur, scale, whole, *chunks):
    vectors = basis.shape[0]
    base = jnp.dot(shared[...], schur[...], preferred_element_type=jnp.float32)
    base = (scale[...] * base).astype(jnp.bfloat16)
    whole[:vectors] = basis[...]
    whole[vectors:] = base
    chunks[0][:vectors] = basis[...]
    row = -vectors
    for chunk in chunks:
        skip = max(-row, 0)
        chunk[skip:] = base[row + skip : row + chunk.shape[0]]
        row += chunk.shape[0]


def share_sources(member, members):
    other = jnp.where(member % 2 == 0, member + members - 1, member + 1) % members
    return ((0, member), (1, member), (2, member), (0, member ^ 1), (0, other))


def solve_kernel(members, vectors, place, weights, *refs):
    *coarse, sent, kept, solved = refs
    me = place[1]
    kb = members * vectors
    total, slot = None, 0
    for ref in coarse:
        for j in range(ref.shape[0]):
            term = jnp.dot(
                weights[:, slot * vectors : (slot + 1) * vectors], ref[j], preferred_element_type=jnp.float32
            )
            total = term if total is None else total + term
            slot += 1
    solved[...] = total
    for j in range(members):
        share = kept if j % 2 == 0 else sent
        for i, (target, member) in enumerate(share_sources(me ^ j, members)):
            start = pl.multiple_of(target * kb + member * vectors, vectors)
            share[j // 2, i * vectors : (i + 1) * vectors] = solved[pl.ds(start, vectors)].astype(jnp.bfloat16)


def sum_kernel(blocks, counts, pick, whole, *refs):
    *pieces, total, basis = refs
    rows, columns = total.shape
    width, vectors = columns // blocks, whole.shape[0] - rows
    fields = [[pieces.pop(0) for _ in range(count)] for count in counts]
    basis[...] = jnp.zeros_like(basis)
    basis[:vectors] = whole[:vectors]
    for n in range(blocks):
        cols = slice(n * width, (n + 1) * width)
        for code, field in enumerate(fields):

            @pl.when(pick[n] == code)
            def _():
                basis[(code + 1) * vectors : (code + 2) * vectors, cols] = field[0][:vectors, cols]
                row = -vectors
                for ref in field:
                    skip = max(-row, 0)
                    place = slice(row + skip, row + ref.shape[0])
                    mine = whole[place.start + vectors : place.stop + vectors, cols].astype(jnp.float32)
                    total[place, cols] = mine + ref[skip:, cols].astype(jnp.float32)
                    row += ref.shape[0]


def last_kernel(total, basis, *refs):
    *lifted, out = refs
    left = lifted[0][...].astype(jnp.float32)
    for ref in lifted[1:]:
        left = left + ref[...].astype(jnp.float32)
    change = jnp.dot(left.astype(jnp.bfloat16).T, basis[...], preferred_element_type=jnp.float32)
    out[...] = (total[...] + change).astype(jnp.bfloat16)


def call(kernel, shapes, in_specs, scratch, cost, *args):
    single = not isinstance(shapes, (list, tuple))
    return pl.pallas_call(
        kernel,
        out_shape=shapes,
        in_specs=in_specs,
        out_specs=VMEM if single else [VMEM] * len(shapes),
        scratch_shapes=scratch,
        compiler_params=pltpu.CompilerParams(vmem_limit_bytes=12 << 20),
        cost_estimate=pl.CostEstimate(flops=cost, bytes_accessed=1 << 20, transcendentals=0),
    )(*args)


def solved_by_ring(coarse, panel, inverse):
    groups = lax.axis_size("grp")
    start = coarse.astype(jnp.float32)
    panel, inverse = panel.astype(jnp.float32).T, inverse.astype(jnp.float32).T

    def advance(step, state):
        received = lax.ppermute(state, "grp", [(i, i + 1) for i in range(groups - 1)])
        return start + exact(panel, received)

    carried = lax.fori_loop(0, groups - 1, advance, start)
    solved = exact(inverse, carried).astype(jnp.bfloat16)
    return jnp.concatenate([solved, swap(solved, "grp", near), swap(solved, "grp", far(groups))])


def lifted_by_ring(restricted, panel, inverse, members):
    vectors, rows = restricted.shape
    part = rows // members
    payload = restricted.reshape(vectors, members, part).transpose(1, 0, 2)
    coarse = lax.all_to_all(payload, "sub", 0, 0).reshape(members * vectors, part)
    solved = solved_by_ring(coarse, panel, inverse).reshape(3, members, vectors, part)
    sub_far = far(members)
    shares = jnp.stack(
        [
            jnp.concatenate([solved[0, m], solved[1, m], solved[2, m], solved[0, near(m)], solved[0, sub_far(m)]])
            for m in range(members)
        ]
    )
    return lax.all_to_all(shares, "sub", 0, 0).transpose(1, 0, 2).reshape(5 * vectors, rows)


def body(resid, neighbour_map, schur, deflation, forward_panels, block_inverses, scaling):
    groups, members = lax.axis_size("grp"), lax.axis_size("sub")
    field, defl, local_schur, scale = resid[0, 0], deflation[0, 0], schur[0, 0], scaling[0]
    rows, columns = field.shape
    vectors = defl.shape[0]
    blocks = neighbour_map.shape[-1]
    pick = chosen(neighbour_map)
    sub_far = far(members)
    bf16 = functools.partial(jax.ShapeDtypeStruct, dtype=jnp.bfloat16)

    near_g, low = [], 0
    for size in chunk_sizes(rows, CUTS_ONE):
        near_g.append(swap(field[low : low + size], "grp", near))
        low += size
    far_m = swap(field, "sub", sub_far)
    near_m = swap(field, "sub", near)
    far_g = [swap(piece, "grp", onward(groups)) for piece in near_g]

    here, member = lax.axis_index("grp"), lax.axis_index("sub")
    step = jnp.where(here % 2 == 0, 1, -1)
    targets = (here, (here + step) % groups, (here - step) % groups)
    gathered = groups * block_inverses.size * len(targets) <= MOST_WEIGHTS and groups & (groups - 1) == 0 and members == 4
    if gathered:
        weights = coarse_weights(forward_panels, block_inverses, targets, vectors)

    shared, restricted = call(
        functools.partial(join_kernel, blocks, (len(near_g), len(far_g), 1, 1)),
        [bf16((rows, columns)), bf16((1, vectors, rows))],
        [SMEM] + [VMEM] * (4 + len(near_g) + len(far_g)),
        [],
        2 * rows * columns * vectors,
        pick, field, defl, *near_g, *far_g, near_m, far_m,
    )
    basis = call(
        basis_kernel,
        bf16((vectors, columns)),
        [VMEM] * 3,
        [],
        2 * vectors * columns * columns,
        defl, local_schur, scale,
    )
    sizes = chunk_sizes(rows, CUTS_TWO)
    sizes[0] += vectors
    whole, *chunks = call(
        base_kernel,
        [bf16((vectors + rows, columns))] + [bf16((size, columns)) for size in sizes],
        [VMEM] * 4,
        [],
        2 * rows * columns * columns,
        shared, basis, local_schur, scale,
    )
    two_near_g = [swap(chunk, "grp", near) for chunk in chunks]
    two_far_g = [swap(chunk, "grp", onward(groups)) for chunk in two_near_g]
    two_near_m = swap(whole, "sub", near)
    two_far_m = swap(whole, "sub", sub_far)

    if gathered:
        pieces = [restricted]
        for bit in bits_of(groups):
            stack = jnp.concatenate(pieces) if len(pieces) > 1 else restricted
            pieces.append(swap(stack, "grp", lambda i: i ^ bit))
        half = (members // 2, 5 * vectors, rows)
        sent, kept = call(
            functools.partial(solve_kernel, members, vectors),
            [bf16(half), bf16(half)],
            [SMEM] + [VMEM] * (1 + len(pieces)),
            [pltpu.VMEM((weights.shape[0], rows), jnp.float32)],
            2 * weights.size * rows,
            jnp.stack([here, member]).astype(jnp.int32), weights, *pieces,
        )
        came = swap(sent, "sub", near)
        passed = (kept[1].astype(jnp.float32) + came[1].astype(jnp.float32)).astype(jnp.bfloat16)
        lifted = [kept[0], came[0], swap(passed, "sub", lambda i: i ^ 2)]
    else:
        lifted = [lifted_by_ring(restricted[0], forward_panels[0], block_inverses[0], members)]

    total, masked = call(
        functools.partial(sum_kernel, blocks, (len(two_near_g), len(two_far_g), 1, 1)),
        [jax.ShapeDtypeStruct((rows, columns), jnp.float32), bf16((5 * vectors, columns))],
        [SMEM] + [VMEM] * (3 + len(two_near_g) + len(two_far_g)),
        [],
        rows * columns,
        pick, whole, *two_near_g, *two_far_g, two_near_m, two_far_m,
    )
    out = call(
        last_kernel,
        bf16((rows, columns)),
        [VMEM] * (2 + len(lifted)),
        [],
        10 * vectors * rows * columns,
        total, masked, *lifted,
    )
    return out[None, None]


def solution(mesh):
    return jax.shard_map(
        body,
        mesh=mesh,
        in_specs=(
            P("grp", "sub", None, None),
            P("grp", "sub", None),
            P("grp", "sub", None, None),
            P("grp", "sub", None, None),
            P("grp", None, None),
            P("grp", None, None),
            P("grp", "sub", None),
        ),
        out_specs=P("grp", "sub", None, None),
        check_vma=False,
    )
```

time: 125 us -> 72.8 us (0.58)
  starting transfers between devices: 54.7 us -> 25 us
  waiting for transfers between devices: 61 us -> 37 us
  Pallas kernels: 0 us -> 7.51 us
  matrix products: 3.7 us -> 0 us
  other arithmetic: 3.46 us -> 0.23 us
  local copies, waits for them, and re-layouts: 1.27 us -> 2.66 us
    ppermute x15 -> x22, starting transfers between devices: 48 us -> 25 us  [swap(): return lax.ppermute(block, axis, route)]
    ppermute x15 -> x22, waiting for transfers between devices: 53.6 us -> 37 us  [swap(): return lax.ppermute(block, axis, route)]
    pallas_call x0 -> x7, Pallas kernels: none -> 7.51 us  [call(): pl.pallas_call(kernel, out_shape=shapes, in_specs=in_specs, out_specs=VME...]
    all_to_all x2 -> x0, waiting for transfers between devices: 7.35 us -> none  [the longest x1 3.89 us: body(): lax.all_to_all(restricted.astype(jnp.bfloat16), 'sub', split_axis=0, conc...]
    all_to_all x2 -> x0, starting transfers between devices: 6.66 us -> none  [the longest x1 3.4 us: body(): lax.all_to_all(restricted.astype(jnp.bfloat16), 'sub', split_axis=0, conc...]
    dot_general x12 -> x0, matrix products: 3.7 us -> none  [the longest x9 2.59 us: product(): return jnp.dot(left, right, precision=lax.Precision.HIGHEST)]
    squeeze x1 -> x0, other arithmetic: 1.53 us -> none  [body(): local_rows = shared[0, 0]]
  transfers between devices with their start and end apart: 17 -> 22, of which waited for: 13 -> 10; matrix products, arithmetic and copies ran while one was open for 1% -> 2% of each run, Pallas kernels for 0% -> 9%
where the time goes in v1:
time: 72.8 us; the launch traced here: 72.5 us
  waiting for transfers between devices  37 us (51%)
  starting transfers between devices  25 us (34%)
  Pallas kernels  7.51 us (10%)
  local copies, waits for them, and re-layouts  2.66 us (4%)
    ppermute x22, waiting for transfers between devices, swap(): return lax.ppermute(block, axis, route)  37 us
    ppermute x22, starting transfers between devices, swap(): return lax.ppermute(block, axis, route)  25 us
    pallas_call x7, Pallas kernels, call(): pl.pallas_call(kernel, out_shape=shapes, in_specs=in_specs, out_specs=VME...  7.51 us
    unnamed x14, local copies, waits for them, and re-layouts  1.49 us
  transfers between devices with their start and end apart: 22, of which 10 were waited for; matrix products, arithmetic and copies ran while one was open for 2% of the time, Pallas kernels for 9%

profile of v1, /device:TPU:0, one launch (start us, length us, event | category | flops | bytes accessed | tf_op | source)
XLA Modules:
  0.0 72.5 jit_solution(2761611125192338953)
XLA Ops:
  0.5 2.6 %collective-permute-start.5 = (bf16[512,512]{1,0:T(8,128)(2,1)}, bf16[512,512]{1,0:T(8,128)(2,1)S(1)}, u32[]{:S(2)}, u32[]{:S(2)}) collective-permute-start(bf16[512,512]{1,0:T(8,128)(2,1)} %bitcast.31), channel_id=1, source_target_pairs={{0,3},{1,2},{2,1},{3,0},{4,7},{5,6},{6,5},{7,4},{8,11},{9,10},{10,... | collective-permute-start | bytes 1572872 | tf_op jit(solution)/shard_map/ppermute | solution.py:20
  3.1 1.1 %slice_bitcast_fusion = (bf16[256,512]{1,0:T(8,128)(2,1)S(1)}, bf16[256,512]{1,0:T(8,128)(2,1)S(1)}) fusion(bf16[1,1,512,512]{3,2,1,0:T(8,128)(2,1)} %param.7), kind=kLoop, calls=%fused_computation.2 | loop fusion | bytes 1048576 | tf_op jit(solution)/shard_map/slice | solution.py:267
  4.2 1.6 %collective-permute-start = (bf16[256,512]{1,0:T(8,128)(2,1)S(1)}, bf16[256,512]{1,0:T(8,128)(2,1)S(1)}, u32[]{:S(2)}, u32[]{:S(2)}) collective-permute-start(bf16[256,512]{1,0:T(8,128)(2,1)S(1)} %get-tuple-element.24), channel_id=1, source_target_pairs={{0,4},{4,0},{8,12},{12,8},{16,20},{20,16},{24,28},{28,24},{1,5},{5... | collective-permute-start | bytes 786440 | tf_op jit(solution)/shard_map/ppermute | solution.py:20
  7.1 1.6 %collective-permute-start.12 = (bf16[1,64,128]{2,1,0:T(8,128)(2,1)S(1)}, bf16[1,64,128]{2,1,0:T(8,128)(2,1)S(1)}, u32[]{:S(2)}, u32[]{:S(2)}) collective-permute-start(bf16[1,64,128]{2,1,0:T(8,128)(2,1)S(1)} %slice_select_fusion), channel_id=1, source_target_pairs={{0,8},{4,12},{8,0},{12,4},{16,24},{20,28},{24,16},{28,20},{1,9},{5... | collective-permute-start | bytes 49160 | tf_op jit(solution)/shard_map/ppermute | solution.py:20
  8.7 2.2 %collective-permute-done.12 = bf16[1,64,128]{2,1,0:T(8,128)(2,1)S(1)} collective-permute-done((bf16[1,64,128]{2,1,0:T(8,128)(2,1)S(1)}, bf16[1,64,128]{2,1,0:T(8,128)(2,1)S(1)}, u32[]{:S(2)}, u32[]{:S(2)}) %collective-permute-start.12) | collective-permute-done | bytes 16416 | tf_op jit(solution)/shard_map/ppermute | solution.py:20
  10.9 2.6 %collective-permute-start.13 = (bf16[2,64,128]{2,1,0:T(8,128)(2,1)S(1)}, bf16[2,64,128]{2,1,0:T(8,128)(2,1)S(1)}, u32[]{:S(2)}, u32[]{:S(2)}) collective-permute-start(bf16[2,64,128]{2,1,0:T(8,128)(2,1)S(1)} %pad_maximum_fusion.5), channel_id=1, source_target_pairs={{0,16},{4,20},{8,24},{12,28},{16,0},{20,4},{24,8},{28,12},{1,17},{... | collective-permute-start | bytes 98312 | tf_op jit(solution)/shard_map/ppermute | solution.py:20
  13.5 1.6 %collective-permute-start.2 = (bf16[256,512]{1,0:T(8,128)(2,1)S(1)}, bf16[256,512]{1,0:T(8,128)(2,1)S(1)}, u32[]{:S(2)}, u32[]{:S(2)}) collective-permute-start(bf16[256,512]{1,0:T(8,128)(2,1)S(1)} %collective-permute-done.refs_0_), channel_id=1, source_target_pairs={{0,8},{4,28},{8,16},{12,4},{16,24},{20,12},{24,0},{28,20},{1,9},{5... | collective-permute-start | bytes 786440 | tf_op jit(solution)/shard_map/ppermute | solution.py:20
  15.0 3.1 %collective-permute-done.1.refs_1_ = bf16[256,512]{1,0:T(8,128)(2,1)S(1)} collective-permute-done((bf16[256,512]{1,0:T(8,128)(2,1)S(1)}, bf16[256,512]{1,0:T(8,128)(2,1)S(1)}, u32[]{:S(2)}, u32[]{:S(2)}) %collective-permute-start.1) | collective-permute-done | bytes 262176 | tf_op jit(solution)/shard_map/ppermute | solution.py:20
  18.1 1.6 %collective-permute-start.3 = (bf16[256,512]{1,0:T(8,128)(2,1)S(1)}, bf16[256,512]{1,0:T(8,128)(2,1)S(1)}, u32[]{:S(2)}, u32[]{:S(2)}) collective-permute-start(bf16[256,512]{1,0:T(8,128)(2,1)S(1)} %collective-permute-done.1.refs_1_), channel_id=1, source_target_pairs={{0,8},{4,28},{8,16},{12,4},{16,24},{20,12},{24,0},{28,20},{1,9},{5... | collective-permute-start | bytes 786440 | tf_op jit(solution)/shard_map/ppermute | solution.py:20
  19.7 3.6 %collective-permute-start.14 = (bf16[4,64,128]{2,1,0:T(8,128)(2,1)S(1)}, bf16[4,64,128]{2,1,0:T(8,128)(2,1)S(1)}, u32[]{:S(2)}, u32[]{:S(2)}) collective-permute-start(bf16[4,64,128]{2,1,0:T(8,128)(2,1)S(1)} %pad_maximum_fusion.3), channel_id=1, source_target_pairs={{0,4},{4,0},{8,12},{12,8},{16,20},{20,16},{24,28},{28,24},{1,5},{5... | collective-permute-start | bytes 196616 | tf_op jit(solution)/shard_map/ppermute | solution.py:20
  23.3 4.5 %collective-permute-done.3.refs_3_ = bf16[256,512]{1,0:T(8,128)(2,1)S(1)} collective-permute-done((bf16[256,512]{1,0:T(8,128)(2,1)S(1)}, bf16[256,512]{1,0:T(8,128)(2,1)S(1)}, u32[]{:S(2)}, u32[]{:S(2)}) %collective-permute-start.3) | collective-permute-done | bytes 262176 | tf_op jit(solution)/shard_map/ppermute | solution.py:20
  27.8 1.0 %shard_map.73 = (bf16[512,512]{1,0:T(8,128)(2,1)S(1)}, bf16[1,32,512]{2,1,0:T(8,128)(2,1)S(1)}) custom-call(s32[4]{0:T(128)S(1)} %bitcast_select_fusion.pick, bf16[512,512]{1,0:T(8,128)(2,1)S(1)} %bitcast.32, bf16[32,512]{1,0:T(8,128)(2,1)S(1)} %bitcast.33, bf16[256,512]{1,0:T(8,128)(2,1)S(1)} %collective-permute-done.refs_0_, ...), custom_call_target="tpu_custom_call" | custom-call | flops 16777216 | bytes 1048576 | tf_op jit(solution)/shard_map/pallas_call | solution.py:214
  29.7 3.2 %collective-permute-done.17.refs_1_ = bf16[1,32,512]{2,1,0:T(8,128)(2,1)S(1)} collective-permute-done((bf16[1,32,512]{2,1,0:T(8,128)(2,1)S(1)}, bf16[1,32,512]{2,1,0:T(8,128)(2,1)S(1)}, u32[]{:S(2)}, u32[]{:S(2)}) %collective-permute-start.17) | collective-permute-done | bytes 32800 | tf_op jit(solution)/shard_map/ppermute | solution.py:20
  32.9 1.1 %collective-permute-start.18 = (bf16[2,32,512]{2,1,0:T(8,128)(2,1)S(1)}, bf16[2,32,512]{2,1,0:T(8,128)(2,1)S(1)}, u32[]{:S(2)}, u32[]{:S(2)}) collective-permute-start(bf16[2,32,512]{2,1,0:T(8,128)(2,1)S(1)} %pad_maximum_fusion.4), channel_id=1, source_target_pairs={{0,16},{4,20},{8,24},{12,28},{16,0},{20,4},{24,8},{28,12},{1,17},{... | collective-permute-start | bytes 196616 | tf_op jit(solution)/shard_map/ppermute | solution.py:20
  35.2 3.1 %collective-permute-done.18.refs_2_ = bf16[2,32,512]{2,1,0:T(8,128)(2,1)S(1)} collective-permute-done((bf16[2,32,512]{2,1,0:T(8,128)(2,1)S(1)}, bf16[2,32,512]{2,1,0:T(8,128)(2,1)S(1)}, u32[]{:S(2)}, u32[]{:S(2)}) %collective-permute-start.18) | collective-permute-done | bytes 65568 | tf_op jit(solution)/shard_map/ppermute | solution.py:20
  38.6 2.3 %shard_map.77.weights = bf16[384,256]{1,0:T(8,128)(2,1)S(1)} custom-call(s32[5]{0:T(128)S(1)} %stack.35.place, bf16[2,8,64,128]{3,2,1,0:T(8,128)(2,1)S(1)} %pad_maximum_fusion.stack, bf16[2,8,64,128]{3,2,1,0:T(8,128)(2,1)S(1)} %collective-permute-done.16.other), custom_call_target="tpu_custom_call" | custom-call | flops 201326592 | bytes 1048576 | tf_op jit(solution)/shard_map/pallas_call | solution.py:214
  41.4 1.9 %collective-permute-start.7 = (bf16[320,512]{1,0:T(8,128)(2,1)S(1)}, bf16[320,512]{1,0:T(8,128)(2,1)S(1)}, u32[]{:S(2)}, u32[]{:S(2)}) collective-permute-start(bf16[320,512]{1,0:T(8,128)(2,1)S(1)} %get-tuple-element.17), channel_id=1, source_target_pairs={{0,4},{4,0},{8,12},{12,8},{16,20},{20,16},{24,28},{28,24},{1,5},{5... | collective-permute-start | bytes 983048 | tf_op jit(solution)/shard_map/ppermute | solution.py:20
  43.6 1.6 %shard_map.78 = (bf16[2,160,512]{2,1,0:T(8,128)(2,1)S(1)}, bf16[2,160,512]{2,1,0:T(8,128)(2,1)S(1)}) custom-call(s32[2]{0:T(128)S(1)} %pad_add_fusion.place, bf16[384,256]{1,0:T(8,128)(2,1)S(1)} %shard_map.77.weights, bf16[1,32,512]{2,1,0:T(8,128)(2,1)S(1)} %get-tuple-element.20.refs_0_, bf16[1,32,512]{2,1,0:T(8,128)(2,1)S(1)} %collective-permute-done.17.refs_1_, ...), custom_call_target="tpu_custom_call" | custom-call | flops 100663296 | bytes 1048576 | tf_op jit(solution)/shard_map/pallas_call | solution.py:214
  46.1 9.1 %collective-permute-done.6.refs_0_ = bf16[224,512]{1,0:T(8,128)(2,1)S(1)} collective-permute-done((bf16[224,512]{1,0:T(8,128)(2,1)S(1)}, bf16[224,512]{1,0:T(8,128)(2,1)S(1)}, u32[]{:S(2)}, u32[]{:S(2)}) %collective-permute-start.6) | collective-permute-done | bytes 229408 | tf_op jit(solution)/shard_map/ppermute | solution.py:20
  55.3 1.7 %collective-permute-start.8 = (bf16[224,512]{1,0:T(8,128)(2,1)S(1)}, bf16[224,512]{1,0:T(8,128)(2,1)S(1)}, u32[]{:S(2)}, u32[]{:S(2)}) collective-permute-start(bf16[224,512]{1,0:T(8,128)(2,1)S(1)} %collective-permute-done.6.refs_0_), channel_id=1, source_target_pairs={{0,8},{4,28},{8,16},{12,4},{16,24},{20,12},{24,0},{28,20},{1,9},{5... | collective-permute-start | bytes 688136 | tf_op jit(solution)/shard_map/ppermute | solution.py:20
  57.0 1.6 %collective-permute-start.9 = (bf16[320,512]{1,0:T(8,128)(2,1)S(1)}, bf16[320,512]{1,0:T(8,128)(2,1)S(1)}, u32[]{:S(2)}, u32[]{:S(2)}) collective-permute-start(bf16[320,512]{1,0:T(8,128)(2,1)S(1)} %collective-permute-done.7.refs_1_), channel_id=1, source_target_pairs={{0,8},{4,28},{8,16},{12,4},{16,24},{20,12},{24,0},{28,20},{1,9},{5... | collective-permute-start | bytes 983048 | tf_op jit(solution)/shard_map/ppermute | solution.py:20
  59.3 6.3 %collective-permute-done.8.refs_2_ = bf16[224,512]{1,0:T(8,128)(2,1)S(1)} collective-permute-done((bf16[224,512]{1,0:T(8,128)(2,1)S(1)}, bf16[224,512]{1,0:T(8,128)(2,1)S(1)}, u32[]{:S(2)}, u32[]{:S(2)}) %collective-permute-start.8) | collective-permute-done | bytes 229408 | tf_op jit(solution)/shard_map/ppermute | solution.py:20
  65.6 5.0 %collective-permute-done.9.refs_3_ = bf16[320,512]{1,0:T(8,128)(2,1)S(1)} collective-permute-done((bf16[320,512]{1,0:T(8,128)(2,1)S(1)}, bf16[320,512]{1,0:T(8,128)(2,1)S(1)}, u32[]{:S(2)}, u32[]{:S(2)}) %collective-permute-start.9) | collective-permute-done | bytes 327712 | tf_op jit(solution)/shard_map/ppermute | solution.py:20
  71.4 1.1 %shard_map.79 = bf16[512,512]{1,0:T(8,128)(2,1)} custom-call(f32[512,512]{1,0:T(8,128)S(1)} %get-tuple-element.18.total, bf16[160,512]{1,0:T(8,128)(2,1)S(1)} %get-tuple-element.19.basis, bf16[160,512]{1,0:T(8,128)(2,1)S(1)} %slice_bitcast_fusion.3.refs_0_, bf16[160,512]{1,0:T(8,128)(2,1)S(1)} %slice_bitcast_fusion.2.refs_1_, ...), custom_call_target="tpu_custom_call" | custom-call | flops 83886080 | bytes 1048576 | tf_op jit(solution)/shard_map/pallas_call | solution.py:214
  (56 shorter events, 7.2 us)
Async XLA Ops:
  0.0 27.8 %copy-start.1 = (bf16[1,1,512,512]{3,2,1,0:T(8,128)(2,1)S(1)}, bf16[1,1,512,512]{3,2,1,0:T(8,128)(2,1)}, u32[]{:S(2)}) copy-start(bf16[1,1,512,512]{3,2,1,0:T(8,128)(2,1)} %param.7) | copy-start | bytes 1572868
  0.0 27.8 %collective-permute-start.4 = (bf16[512,512]{1,0:T(8,128)(2,1)}, bf16[512,512]{1,0:T(8,128)(2,1)S(1)}, u32[]{:S(2)}, u32[]{:S(2)}) collective-permute-start(bf16[512,512]{1,0:T(8,128)(2,1)} %bitcast.30), channel_id=1, source_target_pairs={{0,1},{1,0},{2,3},{3,2},{4,5},{5,4},{6,7},{7,6},{8,9},{9,8},{10,11... | collective-permute-start | bytes 1572872 | tf_op jit(solution)/shard_map/ppermute | solution.py:20
  0.5 27.3 %collective-permute-start.5 = (bf16[512,512]{1,0:T(8,128)(2,1)}, bf16[512,512]{1,0:T(8,128)(2,1)S(1)}, u32[]{:S(2)}, u32[]{:S(2)}) collective-permute-start(bf16[512,512]{1,0:T(8,128)(2,1)} %bitcast.31), channel_id=1, source_target_pairs={{0,3},{1,2},{2,1},{3,0},{4,7},{5,6},{6,5},{7,4},{8,11},{9,10},{10,... | collective-permute-start | bytes 1572872 | tf_op jit(solution)/shard_map/ppermute | solution.py:20
  4.2 9.3 %collective-permute-start = (bf16[256,512]{1,0:T(8,128)(2,1)S(1)}, bf16[256,512]{1,0:T(8,128)(2,1)S(1)}, u32[]{:S(2)}, u32[]{:S(2)}) collective-permute-start(bf16[256,512]{1,0:T(8,128)(2,1)S(1)} %get-tuple-element.24), channel_id=1, source_target_pairs={{0,4},{4,0},{8,12},{12,8},{16,20},{20,16},{24,28},{28,24},{1,5},{5... | collective-permute-start | bytes 786440 | tf_op jit(solution)/shard_map/ppermute | solution.py:20
  5.7 12.4 %collective-permute-start.1 = (bf16[256,512]{1,0:T(8,128)(2,1)S(1)}, bf16[256,512]{1,0:T(8,128)(2,1)S(1)}, u32[]{:S(2)}, u32[]{:S(2)}) collective-permute-start(bf16[256,512]{1,0:T(8,128)(2,1)S(1)} %get-tuple-element.23), channel_id=1, source_target_pairs={{0,4},{4,0},{8,12},{12,8},{16,20},{20,16},{24,28},{28,24},{1,5},{5... | collective-permute-start | bytes 786440 | tf_op jit(solution)/shard_map/ppermute | solution.py:20
  7.1 3.8 %collective-permute-start.12 = (bf16[1,64,128]{2,1,0:T(8,128)(2,1)S(1)}, bf16[1,64,128]{2,1,0:T(8,128)(2,1)S(1)}, u32[]{:S(2)}, u32[]{:S(2)}) collective-permute-start(bf16[1,64,128]{2,1,0:T(8,128)(2,1)S(1)} %slice_select_fusion), channel_id=1, source_target_pairs={{0,8},{4,12},{8,0},{12,4},{16,24},{20,28},{24,16},{28,20},{1,9},{5... | collective-permute-start | bytes 49160 | tf_op jit(solution)/shard_map/ppermute | solution.py:20
  10.9 8.8 %collective-permute-start.13 = (bf16[2,64,128]{2,1,0:T(8,128)(2,1)S(1)}, bf16[2,64,128]{2,1,0:T(8,128)(2,1)S(1)}, u32[]{:S(2)}, u32[]{:S(2)}) collective-permute-start(bf16[2,64,128]{2,1,0:T(8,128)(2,1)S(1)} %pad_maximum_fusion.5), channel_id=1, source_target_pairs={{0,16},{4,20},{8,24},{12,28},{16,0},{20,4},{24,8},{28,12},{1,17},{... | collective-permute-start | bytes 98312 | tf_op jit(solution)/shard_map/ppermute | solution.py:20
  13.5 14.4 %copy-start.2 = (bf16[1,1,32,512]{3,2,1,0:T(8,128)(2,1)S(1)}, bf16[1,1,32,512]{3,2,1,0:T(8,128)(2,1)}, u32[]{:S(2)}) copy-start(bf16[1,1,32,512]{3,2,1,0:T(8,128)(2,1)} %param.10) | copy-start | bytes 98308
  13.5 9.9 %collective-permute-start.2 = (bf16[256,512]{1,0:T(8,128)(2,1)S(1)}, bf16[256,512]{1,0:T(8,128)(2,1)S(1)}, u32[]{:S(2)}, u32[]{:S(2)}) collective-permute-start(bf16[256,512]{1,0:T(8,128)(2,1)S(1)} %collective-permute-done.refs_0_), channel_id=1, source_target_pairs={{0,8},{4,28},{8,16},{12,4},{16,24},{20,12},{24,0},{28,20},{1,9},{5... | collective-permute-start | bytes 786440 | tf_op jit(solution)/shard_map/ppermute | solution.py:20
  18.1 9.7 %collective-permute-start.3 = (bf16[256,512]{1,0:T(8,128)(2,1)S(1)}, bf16[256,512]{1,0:T(8,128)(2,1)S(1)}, u32[]{:S(2)}, u32[]{:S(2)}) collective-permute-start(bf16[256,512]{1,0:T(8,128)(2,1)S(1)} %collective-permute-done.1.refs_1_), channel_id=1, source_target_pairs={{0,8},{4,28},{8,16},{12,4},{16,24},{20,12},{24,0},{28,20},{1,9},{5... | collective-permute-start | bytes 786440 | tf_op jit(solution)/shard_map/ppermute | solution.py:20
  19.7 9.3 %collective-permute-start.14 = (bf16[4,64,128]{2,1,0:T(8,128)(2,1)S(1)}, bf16[4,64,128]{2,1,0:T(8,128)(2,1)S(1)}, u32[]{:S(2)}, u32[]{:S(2)}) collective-permute-start(bf16[4,64,128]{2,1,0:T(8,128)(2,1)S(1)} %pad_maximum_fusion.3), channel_id=1, source_target_pairs={{0,4},{4,0},{8,12},{12,8},{16,20},{20,16},{24,28},{28,24},{1,5},{5... | collective-permute-start | bytes 196616 | tf_op jit(solution)/shard_map/ppermute | solution.py:20
  28.9 4.0 %collective-permute-start.17 = (bf16[1,32,512]{2,1,0:T(8,128)(2,1)S(1)}, bf16[1,32,512]{2,1,0:T(8,128)(2,1)S(1)}, u32[]{:S(2)}, u32[]{:S(2)}) collective-permute-start(bf16[1,32,512]{2,1,0:T(8,128)(2,1)S(1)} %get-tuple-element.20.refs_0_), channel_id=1, source_target_pairs={{0,8},{4,12},{8,0},{12,4},{16,24},{20,28},{24,16},{28,20},{1,9},{5... | collective-permute-start | bytes 98312 | tf_op jit(solution)/shard_map/ppermute | solution.py:20
  29.0 5.0 %collective-permute-start.15 = (bf16[8,64,128]{2,1,0:T(8,128)(2,1)S(1)}, bf16[8,64,128]{2,1,0:T(8,128)(2,1)S(1)}, u32[]{:S(2)}, u32[]{:S(2)}) collective-permute-start(bf16[8,64,128]{2,1,0:T(8,128)(2,1)S(1)} %get-tuple-element.26), channel_id=1, source_target_pairs={{0,2},{1,3},{2,0},{3,1},{4,6},{5,7},{6,4},{7,5},{8,10},{9,11},{10,... | collective-permute-start | bytes 393224 | tf_op jit(solution)/shard_map/ppermute | solution.py:20
  32.9 5.4 %collective-permute-start.18 = (bf16[2,32,512]{2,1,0:T(8,128)(2,1)S(1)}, bf16[2,32,512]{2,1,0:T(8,128)(2,1)S(1)}, u32[]{:S(2)}, u32[]{:S(2)}) collective-permute-start(bf16[2,32,512]{2,1,0:T(8,128)(2,1)S(1)} %pad_maximum_fusion.4), channel_id=1, source_target_pairs={{0,16},{4,20},{8,24},{12,28},{16,0},{20,4},{24,8},{28,12},{1,17},{... | collective-permute-start | bytes 196616 | tf_op jit(solution)/shard_map/ppermute | solution.py:20
  34.1 4.5 %collective-permute-start.16 = (bf16[2,8,64,128]{3,2,1,0:T(8,128)(2,1)S(1)}, bf16[2,8,64,128]{3,2,1,0:T(8,128)(2,1)S(1)}, u32[]{:S(2)}, u32[]{:S(2)}) collective-permute-start(bf16[2,8,64,128]{3,2,1,0:T(8,128)(2,1)S(1)} %pad_maximum_fusion.stack), channel_id=1, source_target_pairs={{0,1},{1,0},{2,3},{3,2},{4,5},{5,4},{6,7},{7,6},{8,9},{9,8},{10,11... | collective-permute-start | bytes 786440 | tf_op jit(solution)/shard_map/ppermute | solution.py:20
  38.3 5.3 %collective-permute-start.19 = (bf16[4,32,512]{2,1,0:T(8,128)(2,1)S(1)}, bf16[4,32,512]{2,1,0:T(8,128)(2,1)S(1)}, u32[]{:S(2)}, u32[]{:S(2)}) collective-permute-start(bf16[4,32,512]{2,1,0:T(8,128)(2,1)S(1)} %pad_maximum_fusion.2), channel_id=1, source_target_pairs={{0,4},{4,0},{8,12},{12,8},{16,20},{20,16},{24,28},{28,24},{1,5},{5... | collective-permute-start | bytes 393224 | tf_op jit(solution)/shard_map/ppermute | solution.py:20
  41.4 15.6 %collective-permute-start.7 = (bf16[320,512]{1,0:T(8,128)(2,1)S(1)}, bf16[320,512]{1,0:T(8,128)(2,1)S(1)}, u32[]{:S(2)}, u32[]{:S(2)}) collective-permute-start(bf16[320,512]{1,0:T(8,128)(2,1)S(1)} %get-tuple-element.17), channel_id=1, source_target_pairs={{0,4},{4,0},{8,12},{12,8},{16,20},{20,16},{24,28},{28,24},{1,5},{5... | collective-permute-start | bytes 983048 | tf_op jit(solution)/shard_map/ppermute | solution.py:20
  45.2 13.4 %collective-permute-start.20 = (bf16[2,160,512]{2,1,0:T(8,128)(2,1)S(1)}, bf16[2,160,512]{2,1,0:T(8,128)(2,1)S(1)}, u32[]{:S(2)}, u32[]{:S(2)}) collective-permute-start(bf16[2,160,512]{2,1,0:T(8,128)(2,1)S(1)} %get-tuple-element.22), channel_id=1, source_target_pairs={{0,1},{1,0},{2,3},{3,2},{4,5},{5,4},{6,7},{7,6},{8,9},{9,8},{10,11... | collective-permute-start | bytes 983048 | tf_op jit(solution)/shard_map/ppermute | solution.py:20
  45.3 20.2 %collective-permute-start.10 = (bf16[544,512]{1,0:T(8,128)(2,1)S(1)}, bf16[544,512]{1,0:T(8,128)(2,1)S(1)}, u32[]{:S(2)}, u32[]{:S(2)}) collective-permute-start(bf16[544,512]{1,0:T(8,128)(2,1)S(1)} %get-tuple-element.15.whole), channel_id=1, source_target_pairs={{0,1},{1,0},{2,3},{3,2},{4,5},{5,4},{6,7},{7,6},{8,9},{9,8},{10,11... | collective-permute-start | bytes 1671176 | tf_op jit(solution)/shard_map/ppermute | solution.py:20
  45.8 19.7 %collective-permute-start.11 = (bf16[544,512]{1,0:T(8,128)(2,1)S(1)}, bf16[544,512]{1,0:T(8,128)(2,1)S(1)}, u32[]{:S(2)}, u32[]{:S(2)}) collective-permute-start(bf16[544,512]{1,0:T(8,128)(2,1)S(1)} %get-tuple-element.15.whole), channel_id=1, source_target_pairs={{0,3},{1,2},{2,1},{3,0},{4,7},{5,6},{6,5},{7,4},{8,11},{9,10},{10,... | collective-permute-start | bytes 1671176 | tf_op jit(solution)/shard_map/ppermute | solution.py:20
  46.1 9.2 %collective-permute-start.6 = (bf16[224,512]{1,0:T(8,128)(2,1)S(1)}, bf16[224,512]{1,0:T(8,128)(2,1)S(1)}, u32[]{:S(2)}, u32[]{:S(2)}) collective-permute-start(bf16[224,512]{1,0:T(8,128)(2,1)S(1)} %get-tuple-element.16), channel_id=1, source_target_pairs={{0,4},{4,0},{8,12},{12,8},{16,20},{20,16},{24,28},{28,24},{1,5},{5... | collective-permute-start | bytes 688136 | tf_op jit(solution)/shard_map/ppermute | solution.py:20
  55.3 10.3 %collective-permute-start.8 = (bf16[224,512]{1,0:T(8,128)(2,1)S(1)}, bf16[224,512]{1,0:T(8,128)(2,1)S(1)}, u32[]{:S(2)}, u32[]{:S(2)}) collective-permute-start(bf16[224,512]{1,0:T(8,128)(2,1)S(1)} %collective-permute-done.6.refs_0_), channel_id=1, source_target_pairs={{0,8},{4,28},{8,16},{12,4},{16,24},{20,12},{24,0},{28,20},{1,9},{5... | collective-permute-start | bytes 688136 | tf_op jit(solution)/shard_map/ppermute | solution.py:20
  57.0 13.6 %collective-permute-start.9 = (bf16[320,512]{1,0:T(8,128)(2,1)S(1)}, bf16[320,512]{1,0:T(8,128)(2,1)S(1)}, u32[]{:S(2)}, u32[]{:S(2)}) collective-permute-start(bf16[320,512]{1,0:T(8,128)(2,1)S(1)} %collective-permute-done.7.refs_1_), channel_id=1, source_target_pairs={{0,8},{4,28},{8,16},{12,4},{16,24},{20,12},{24,0},{28,20},{1,9},{5... | collective-permute-start | bytes 983048 | tf_op jit(solution)/shard_map/ppermute | solution.py:20
  58.7 12.7 %collective-permute-start.21 = (bf16[160,512]{1,0:T(8,128)(2,1)S(1)}, bf16[160,512]{1,0:T(8,128)(2,1)S(1)}, u32[]{:S(2)}, u32[]{:S(2)}) collective-permute-start(bf16[160,512]{1,0:T(8,128)(2,1)S(1)} %fusion), channel_id=1, source_target_pairs={{0,2},{1,3},{2,0},{3,1},{4,6},{5,7},{6,4},{7,5},{8,10},{9,11},{10,... | collective-permute-start | bytes 491528 | tf_op jit(solution)/shard_map/ppermute | solution.py:20
  (5 other events, 17.5 us)

commit v2 on v1

--- a/solution.py
+++ b/solution.py
@@ -10,7 +10,7 @@
 
 MOST_WEIGHTS = 1 << 20
 CUTS_ONE = (4,)
-CUTS_TWO = (3,)
+CUTS_TWO = (4,)
 VMEM = pl.BlockSpec(memory_space=pltpu.VMEM)
 SMEM = pl.BlockSpec(memory_space=pltpu.SMEM)
 
@@ -37,37 +37,39 @@
     return [high - low for low, high in zip(ends, ends[1:])]
 
 
-def chosen(neighbour_map):
-    codes = neighbour_map[0, 0]
-    odd_g, odd_m = lax.axis_index("grp") % 2, lax.axis_index("sub") % 2
-    return jnp.where(codes < 2, (codes + 1 + odd_g) % 2, 2 + (codes + 1 + odd_m) % 2)
+def chosen(codes, n):
+    odd_g, odd_m = lax.rem(lax.axis_index("grp"), 2), lax.rem(lax.axis_index("sub"), 2)
+    code = codes[n]
+    return jnp.where(code < 2, lax.rem(code + 1 + odd_g, 2), 2 + lax.rem(code + 1 + odd_m, 2))
 
 
 def exact(left, right):
     return jnp.dot(left, right, precision=lax.Precision.HIGHEST)
 
 
-def bits_of(groups):
-    bits, bit = [], 2
-    while bit < groups:
-        bits.append(bit)
-        bit *= 2
-    return [*bits, 1]
-
-
-def weights_kernel(groups, vectors, place, stack, other, weights, below, picked):
-    here, member = place[0], place[1]
-    kb = stack.shape[3]
-    targets = [place[2 + i] for i in range(weights.shape[0] // kb)]
-    even, upper = member % 2 == 0, member // 2 % 2 == 0
-
-    def slot(h):
-        offset = h ^ here
-        return sum(((offset // bit) % 2) << k for k, bit in enumerate(bits_of(groups)))
+def gathered_slot(offset, groups):
+    return offset // 2 + offset % 2 * (groups // 2)
+
+
+def share_sources(member, members):
+    other = lax.rem(jnp.where(lax.rem(member, 2) == 0, member + members - 1, member + 1), members)
+    return ((0, member), (1, member), (2, member), (0, member ^ 1), (0, other))
+
+
+def kind_kernel(panel, inverse, kind):
+    kind[...] = jnp.where(lax.rem(lax.axis_index("sub"), 2) == 0, panel[...], inverse[...])
+
+
+def weights_kernel(groups, members, vectors, stack, other, weights, below, picked, turned):
+    here, me = lax.axis_index("grp"), lax.axis_index("sub")
+    kb = members * vectors
+    step = 1 - 2 * lax.rem(here, 2)
+    targets = [here, here + step, lax.rem(here - step + groups, groups)]
+    even = lax.rem(me, 2) == 0
 
     def block(h, mine):
-        own, twin = (jnp.where(mine, stack[i, slot(h)], other[i, slot(h)]) for i in range(2))
-        return jnp.concatenate([jnp.where(upper, own, twin), jnp.where(upper, twin, own)])
+        slot = gathered_slot(h ^ here, groups)
+        return jnp.where(mine, stack[slot], other[slot])
 
     below[...] = jnp.zeros_like(below)
     for h in range(groups - 1, -1, -1):
@@ -85,33 +87,45 @@
             def _():
                 below[:, i * kb : (i + 1) * kb] = block(h, ~even).astype(jnp.float32)
 
-        mine = below[pl.ds(pl.multiple_of(member * vectors, vectors), vectors)]
-        picked[pl.ds(pl.multiple_of(slot(h) * vectors, vectors), vectors)] = mine
-    weights[...] = picked[...].T.astype(jnp.bfloat16)
-
-
-def coarse_weights(forward_panels, block_inverses, targets, vectors):
-    groups, here, member = lax.axis_size("grp"), lax.axis_index("grp"), lax.axis_index("sub")
-    kb = forward_panels.shape[-1]
-    half = kb // 2
-    kind = jnp.where(member % 2 == 0, forward_panels[0], block_inverses[0])
-    stack = jnp.where(member // 2 % 2 == 0, kind[:half], kind[half:])[None]
-    for bit in bits_of(groups):
-        stack = jnp.concatenate([stack, swap(stack, "grp", lambda i: i ^ bit)])
-    stack = jnp.stack([stack, swap(stack, "sub", lambda i: i ^ 2)])
+        slot = gathered_slot(h ^ here, groups)
+        mine = below[pl.ds(pl.multiple_of(me * vectors, vectors), vectors)]
+        picked[pl.ds(pl.multiple_of(slot * vectors, vectors), vectors)] = mine
+    turned[...] = picked[...].T
+    for j in range(members):
+        for i, (target, member) in enumerate(share_sources(me ^ j, members)):
+            start = pl.multiple_of(target * kb + member * vectors, vectors)
+            weights[j, i * vectors : (i + 1) * vectors] = turned[pl.ds(start, vectors)].astype(jnp.bfloat16)
+
+
+def coarse_weights(forward_panels, block_inverses, vectors):
+    groups, members = lax.axis_size("grp"), lax.axis_size("sub")
+    shape = jax.ShapeDtypeStruct(forward_panels.shape, forward_panels.dtype)
+    stack = call(kind_kernel, shape, [VMEM] * 2, [], forward_panels.size, forward_panels, block_inverses)
+    bits, bit = [], 2
+    while bit < groups:
+        bits.append(bit)
+        bit *= 2
+    for bit in (*bits, 1):
+        came = swap(stack, "grp", lambda i: i ^ bit)
+        stack = jnp.concatenate([stack, came])
     other = swap(stack, "sub", near)
-    rows = len(targets) * kb
+    kb = stack.shape[2]
+    width = groups * vectors
     return call(
-        functools.partial(weights_kernel, groups, vectors),
-        jax.ShapeDtypeStruct((rows, groups * vectors), jnp.bfloat16),
-        [SMEM, VMEM, VMEM],
-        [pltpu.VMEM((kb, rows), jnp.float32), pltpu.VMEM((groups * vectors, rows), jnp.float32)],
-        4 * groups * kb * kb * rows,
-        jnp.stack([here, member, *targets]).astype(jnp.int32), stack, other,
-    )
-
-
-def join_kernel(blocks, counts, pick, own, defl, *refs):
+        functools.partial(weights_kernel, groups, members, vectors),
+        jax.ShapeDtypeStruct((members, 5 * vectors, width), jnp.bfloat16),
+        [VMEM, VMEM],
+        [
+            pltpu.VMEM((kb, 3 * kb), jnp.float32),
+            pltpu.VMEM((width, 3 * kb), jnp.float32),
+            pltpu.VMEM((3 * kb, width), jnp.float32),
+        ],
+        12 * groups * kb * kb * kb,
+        stack, other,
+    )
+
+
+def join_kernel(blocks, counts, codes, own, defl, *refs):
     *pieces, shared, restricted = refs
     width = own.shape[1] // blocks
     fields = [[pieces.pop(0) for _ in range(count)] for count in counts]
@@ -119,7 +133,7 @@
         cols = slice(n * width, (n + 1) * width)
         for code, field in enumerate(fields):
 
-            @pl.when(pick[n] == code)
+            @pl.when(chosen(codes, n) == code)
             def _():
                 row = 0
                 for ref in field:
@@ -152,32 +166,16 @@
         row += chunk.shape[0]
 
 
-def share_sources(member, members):
-    other = jnp.where(member % 2 == 0, member + members - 1, member + 1) % members
-    return ((0, member), (1, member), (2, member), (0, member ^ 1), (0, other))
-
-
-def solve_kernel(members, vectors, place, weights, *refs):
-    *coarse, sent, kept, solved = refs
-    me = place[1]
-    kb = members * vectors
-    total, slot = None, 0
-    for ref in coarse:
-        for j in range(ref.shape[0]):
-            term = jnp.dot(
-                weights[:, slot * vectors : (slot + 1) * vectors], ref[j], preferred_element_type=jnp.float32
-            )
-            total = term if total is None else total + term
-            slot += 1
-    solved[...] = total
-    for j in range(members):
-        share = kept if j % 2 == 0 else sent
-        for i, (target, member) in enumerate(share_sources(me ^ j, members)):
-            start = pl.multiple_of(target * kb + member * vectors, vectors)
-            share[j // 2, i * vectors : (i + 1) * vectors] = solved[pl.ds(start, vectors)].astype(jnp.bfloat16)
-
-
-def sum_kernel(blocks, counts, pick, whole, *refs):
+def solve_kernel(weights, *refs):
+    *coarse, sent, kept = refs
+    blocks = [ref[j] for ref in coarse for j in range(ref.shape[0])]
+    coarse_all = jnp.concatenate(blocks)
+    for j in range(weights.shape[0]):
+        share = jnp.dot(weights[j], coarse_all, preferred_element_type=jnp.float32)
+        (kept if j % 2 == 0 else sent)[j // 2] = share.astype(jnp.bfloat16)
+
+
+def sum_kernel(blocks, counts, codes, whole, *refs):
     *pieces, total, basis = refs
     rows, columns = total.shape
     width, vectors = columns // blocks, whole.shape[0] - rows
@@ -188,7 +186,7 @@
         cols = slice(n * width, (n + 1) * width)
         for code, field in enumerate(fields):
 
-            @pl.when(pick[n] == code)
+            @pl.when(chosen(codes, n) == code)
             def _():
                 basis[(code + 1) * vectors : (code + 2) * vectors, cols] = field[0][:vectors, cols]
                 row = -vectors
@@ -217,7 +215,7 @@
         in_specs=in_specs,
         out_specs=VMEM if single else [VMEM] * len(shapes),
         scratch_shapes=scratch,
-        compiler_params=pltpu.CompilerParams(vmem_limit_bytes=12 << 20),
+        compiler_params=pltpu.CompilerParams(vmem_limit_bytes=10 << 20),
         cost_estimate=pl.CostEstimate(flops=cost, bytes_accessed=1 << 20, transcendentals=0),
     )(*args)
 
@@ -258,7 +256,7 @@
     rows, columns = field.shape
     vectors = defl.shape[0]
     blocks = neighbour_map.shape[-1]
-    pick = chosen(neighbour_map)
+    codes = neighbour_map[0, 0]
     sub_far = far(members)
     bf16 = functools.partial(jax.ShapeDtypeStruct, dtype=jnp.bfloat16)
 
@@ -270,12 +268,9 @@
     near_m = swap(field, "sub", near)
     far_g = [swap(piece, "grp", onward(groups)) for piece in near_g]
 
-    here, member = lax.axis_index("grp"), lax.axis_index("sub")
-    step = jnp.where(here % 2 == 0, 1, -1)
-    targets = (here, (here + step) % groups, (here - step) % groups)
-    gathered = groups * block_inverses.size * len(targets) <= MOST_WEIGHTS and groups & (groups - 1) == 0 and members == 4
+    gathered = groups * block_inverses.size * 3 <= MOST_WEIGHTS and groups & (groups - 1) == 0 and members == 4
     if gathered:
-        weights = coarse_weights(forward_panels, block_inverses, targets, vectors)
+        weights = coarse_weights(forward_panels, block_inverses, vectors)
 
     shared, restricted = call(
         functools.partial(join_kernel, blocks, (len(near_g), len(far_g), 1, 1)),
@@ -283,7 +278,7 @@
         [SMEM] + [VMEM] * (4 + len(near_g) + len(far_g)),
         [],
         2 * rows * columns * vectors,
-        pick, field, defl, *near_g, *far_g, near_m, far_m,
+        codes, field, defl, *near_g, *far_g, near_m, far_m,
     )
     basis = call(
         basis_kernel,
@@ -310,17 +305,17 @@
 
     if gathered:
         pieces = [restricted]
-        for bit in bits_of(groups):
-            stack = jnp.concatenate(pieces) if len(pieces) > 1 else restricted
-            pieces.append(swap(stack, "grp", lambda i: i ^ bit))
+        for offset in range(2, groups, 2):
+            pieces.append(swap(restricted, "grp", lambda i: i ^ offset))
+        stack = jnp.concatenate(pieces)
         half = (members // 2, 5 * vectors, rows)
         sent, kept = call(
-            functools.partial(solve_kernel, members, vectors),
+            solve_kernel,
             [bf16(half), bf16(half)],
-            [SMEM] + [VMEM] * (1 + len(pieces)),
-            [pltpu.VMEM((weights.shape[0], rows), jnp.float32)],
+            [VMEM] * 3,
+            [],
             2 * weights.size * rows,
-            jnp.stack([here, member]).astype(jnp.int32), weights, *pieces,
+            weights, stack, swap(stack, "grp", near),
         )
         came = swap(sent, "sub", near)
         passed = (kept[1].astype(jnp.float32) + came[1].astype(jnp.float32)).astype(jnp.bfloat16)
@@ -334,7 +329,7 @@
         [SMEM] + [VMEM] * (3 + len(two_near_g) + len(two_far_g)),
         [],
         rows * columns,
-        pick, whole, *two_near_g, *two_far_g, two_near_m, two_far_m,
+        codes, whole, *two_near_g, *two_far_g, two_near_m, two_far_m,
     )
     out = call(
         last_kernel,

time: 72.8 us -> 81.5 us (1.12)
  starting transfers between devices: 25 us -> 33.7 us
  waiting for transfers between devices: 37 us -> 39.1 us
  Pallas kernels: 7.51 us -> 5.92 us
    ppermute x22, starting transfers between devices: 25 us -> 33.7 us  [swap(): return lax.ppermute(block, axis, route)]
    ppermute x22, waiting for transfers between devices: 37 us -> 39.1 us  [swap(): return lax.ppermute(block, axis, route)]
    pallas_call x7 -> x8, Pallas kernels: 7.51 us -> 5.92 us  [call(): pl.pallas_call(kernel, out_shape=shapes, in_specs=in_specs, out_specs=VME...]
  transfers between devices with their start and end apart: 22 -> 22, of which waited for: 10 -> 10; matrix products, arithmetic and copies ran while one was open for 2% -> 0% of each run, Pallas kernels for 9% -> 5%
where the time goes in v2:
time: 81.5 us; the launch traced here: 81.4 us
  waiting for transfers between devices  39.1 us (48%)
  starting transfers between devices  33.7 us (41%)
  Pallas kernels  5.92 us (7%)
  local copies, waits for them, and re-layouts  2.41 us (3%)
    ppermute x22, waiting for transfers between devices, swap(): return lax.ppermute(block, axis, route)  39.1 us
    ppermute x22, starting transfers between devices, swap(): return lax.ppermute(block, axis, route)  33.7 us
    pallas_call x8, Pallas kernels, call(): pl.pallas_call(kernel, out_shape=shapes, in_specs=in_specs, out_specs=VME...  5.92 us
  transfers between devices with their start and end apart: 22, of which 10 were waited for; matrix products, arithmetic and copies ran while one was open for 0% of the time, Pallas kernels for 5%

profile of v2, /device:TPU:0, one launch (start us, length us, event | category | flops | bytes accessed | tf_op | source)
XLA Modules:
  0.0 81.4 jit_solution(11024957194590473331)
XLA Ops:
  1.1 3.0 %collective-permute-start = (bf16[256,512]{1,0:T(8,128)(2,1)S(1)}, bf16[256,512]{1,0:T(8,128)(2,1)S(1)}, u32[]{:S(2)}, u32[]{:S(2)}) collective-permute-start(bf16[256,512]{1,0:T(8,128)(2,1)S(1)} %get-tuple-element.24), channel_id=1, source_target_pairs={{0,4},{4,0},{8,12},{12,8},{16,20},{20,16},{24,28},{28,24},{1,5},{5... | collective-permute-start | bytes 786440 | tf_op jit(solution)/shard_map/ppermute | solution.py:20
  4.3 2.1 %collective-permute-start.12 = (bf16[1,128,128]{2,1,0:T(8,128)(2,1)S(1)}, bf16[1,128,128]{2,1,0:T(8,128)(2,1)S(1)}, u32[]{:S(2)}, u32[]{:S(2)}) collective-permute-start(bf16[1,128,128]{2,1,0:T(8,128)(2,1)S(1)} %shard_map.77), channel_id=1, source_target_pairs={{0,8},{4,12},{8,0},{12,4},{16,24},{20,28},{24,16},{28,20},{1,9},{5... | collective-permute-start | bytes 98312 | tf_op jit(solution)/shard_map/ppermute | solution.py:20
  6.4 1.6 %collective-permute-start.5 = (bf16[512,512]{1,0:T(8,128)(2,1)S(1)}, bf16[512,512]{1,0:T(8,128)(2,1)S(1)}, u32[]{:S(2)}, u32[]{:S(2)}) collective-permute-start(bf16[512,512]{1,0:T(8,128)(2,1)S(1)} %bitcast.19), channel_id=1, source_target_pairs={{0,3},{1,2},{2,1},{3,0},{4,7},{5,6},{6,5},{7,4},{8,11},{9,10},{10,... | collective-permute-start | bytes 1572872 | tf_op jit(solution)/shard_map/ppermute | solution.py:20
  8.3 3.1 %collective-permute-start.13 = (bf16[2,128,128]{2,1,0:T(8,128)(2,1)S(1)}, bf16[2,128,128]{2,1,0:T(8,128)(2,1)S(1)}, u32[]{:S(2)}, u32[]{:S(2)}) collective-permute-start(bf16[2,128,128]{2,1,0:T(8,128)(2,1)S(1)} %pad_maximum_fusion.2), channel_id=1, source_target_pairs={{0,16},{4,20},{8,24},{12,28},{16,0},{20,4},{24,8},{28,12},{1,17},{... | collective-permute-start | bytes 196616 | tf_op jit(solution)/shard_map/ppermute | solution.py:20
  11.4 2.1 %collective-permute-start.2 = (bf16[256,512]{1,0:T(8,128)(2,1)S(1)}, bf16[256,512]{1,0:T(8,128)(2,1)S(1)}, u32[]{:S(2)}, u32[]{:S(2)}) collective-permute-start(bf16[256,512]{1,0:T(8,128)(2,1)S(1)} %collective-permute-done.refs_0_), channel_id=1, source_target_pairs={{0,8},{4,28},{8,16},{12,4},{16,24},{20,12},{24,0},{28,20},{1,9},{5... | collective-permute-start | bytes 786440 | tf_op jit(solution)/shard_map/ppermute | solution.py:20
  13.4 2.7 %collective-permute-done.1.refs_1_ = bf16[256,512]{1,0:T(8,128)(2,1)S(1)} collective-permute-done((bf16[256,512]{1,0:T(8,128)(2,1)S(1)}, bf16[256,512]{1,0:T(8,128)(2,1)S(1)}, u32[]{:S(2)}, u32[]{:S(2)}) %collective-permute-start.1) | collective-permute-done | bytes 262176 | tf_op jit(solution)/shard_map/ppermute | solution.py:20
  16.1 1.8 %collective-permute-start.3 = (bf16[256,512]{1,0:T(8,128)(2,1)S(1)}, bf16[256,512]{1,0:T(8,128)(2,1)S(1)}, u32[]{:S(2)}, u32[]{:S(2)}) collective-permute-start(bf16[256,512]{1,0:T(8,128)(2,1)S(1)} %collective-permute-done.1.refs_1_), channel_id=1, source_target_pairs={{0,8},{4,28},{8,16},{12,4},{16,24},{20,12},{24,0},{28,20},{1,9},{5... | collective-permute-start | bytes 786440 | tf_op jit(solution)/shard_map/ppermute | solution.py:20
  18.0 3.6 %collective-permute-start.14 = (bf16[4,128,128]{2,1,0:T(8,128)(2,1)S(1)}, bf16[4,128,128]{2,1,0:T(8,128)(2,1)S(1)}, u32[]{:S(2)}, u32[]{:S(2)}) collective-permute-start(bf16[4,128,128]{2,1,0:T(8,128)(2,1)S(1)} %pad_maximum_fusion.1), channel_id=1, source_target_pairs={{0,4},{4,0},{8,12},{12,8},{16,20},{20,16},{24,28},{28,24},{1,5},{5... | collective-permute-start | bytes 393224 | tf_op jit(solution)/shard_map/ppermute | solution.py:20
  21.5 2.9 %collective-permute-done.14 = bf16[4,128,128]{2,1,0:T(8,128)(2,1)S(1)} collective-permute-done((bf16[4,128,128]{2,1,0:T(8,128)(2,1)S(1)}, bf16[4,128,128]{2,1,0:T(8,128)(2,1)S(1)}, u32[]{:S(2)}, u32[]{:S(2)}) %collective-permute-start.14) | collective-permute-done | bytes 131104 | tf_op jit(solution)/shard_map/ppermute | solution.py:20
  24.6 1.6 %collective-permute-done.3.refs_3_ = bf16[256,512]{1,0:T(8,128)(2,1)S(1)} collective-permute-done((bf16[256,512]{1,0:T(8,128)(2,1)S(1)}, bf16[256,512]{1,0:T(8,128)(2,1)S(1)}, u32[]{:S(2)}, u32[]{:S(2)}) %collective-permute-start.3) | collective-permute-done | bytes 262176 | tf_op jit(solution)/shard_map/ppermute | solution.py:20
  26.9 1.1 %shard_map.73 = (bf16[512,512]{1,0:T(8,128)(2,1)S(1)}, bf16[1,32,512]{2,1,0:T(8,128)(2,1)S(1)}) custom-call(s32[4]{0:T(128)S(1)} %bitcast.25, bf16[512,512]{1,0:T(8,128)(2,1)S(1)} %bitcast.20, bf16[32,512]{1,0:T(8,128)(2,1)S(1)} %bitcast.21, bf16[256,512]{1,0:T(8,128)(2,1)S(1)} %collective-permute-done.refs_0_, ...), custom_call_target="tpu_custom_call" | custom-call | flops 16777216 | bytes 1048576 | tf_op jit(solution)/shard_map/pallas_call | solution.py:212
  28.1 8.4 %collective-permute-start.17 = (bf16[1,32,512]{2,1,0:T(8,128)(2,1)S(1)}, bf16[1,32,512]{2,1,0:T(8,128)(2,1)S(1)}, u32[]{:S(2)}, u32[]{:S(2)}) collective-permute-start(bf16[1,32,512]{2,1,0:T(8,128)(2,1)S(1)} %get-tuple-element.20), channel_id=1, source_target_pairs={{0,16},{4,20},{8,24},{12,28},{16,0},{20,4},{24,8},{28,12},{1,17},{... | collective-permute-start | bytes 98312 | tf_op jit(solution)/shard_map/ppermute | solution.py:20
  36.5 2.6 %collective-permute-done.17 = bf16[1,32,512]{2,1,0:T(8,128)(2,1)S(1)} collective-permute-done((bf16[1,32,512]{2,1,0:T(8,128)(2,1)S(1)}, bf16[1,32,512]{2,1,0:T(8,128)(2,1)S(1)}, u32[]{:S(2)}, u32[]{:S(2)}) %collective-permute-start.17) | collective-permute-done | bytes 32800 | tf_op jit(solution)/shard_map/ppermute | solution.py:20
  39.1 3.1 %collective-permute-done.18 = bf16[1,32,512]{2,1,0:T(8,128)(2,1)S(1)} collective-permute-done((bf16[1,32,512]{2,1,0:T(8,128)(2,1)S(1)}, bf16[1,32,512]{2,1,0:T(8,128)(2,1)S(1)}, u32[]{:S(2)}, u32[]{:S(2)}) %collective-permute-start.18) | collective-permute-done | bytes 32800 | tf_op jit(solution)/shard_map/ppermute | solution.py:20
  42.2 2.0 %collective-permute-start.19 = (bf16[4,32,512]{2,1,0:T(8,128)(2,1)S(1)}, bf16[4,32,512]{2,1,0:T(8,128)(2,1)S(1)}, u32[]{:S(2)}, u32[]{:S(2)}) collective-permute-start(bf16[4,32,512]{2,1,0:T(8,128)(2,1)S(1)} %constant_dynamic-update-slice_fusion.refs_0_), channel_id=1, source_target_pairs={{0,4},{4,0},{8,12},{12,8},{16,20},{20,16},{24,28},{28,24},{1,5},{5... | collective-permute-start | bytes 393224 | tf_op jit(solution)/shard_map/ppermute | solution.py:20
  44.2 1.7 %shard_map.78.weights = bf16[4,160,256]{2,1,0:T(8,128)(2,1)S(1)} custom-call(bf16[8,128,128]{2,1,0:T(8,128)(2,1)S(1)} %pad_maximum_fusion.stack, bf16[8,128,128]{2,1,0:T(8,128)(2,1)S(1)} %collective-permute-done.15.other), custom_call_target="tpu_custom_call" | custom-call | flops 201326592 | bytes 1048576 | tf_op jit(solution)/shard_map/pallas_call | solution.py:212
  46.0 1.2 %collective-permute-done.19.refs_1_ = bf16[4,32,512]{2,1,0:T(8,128)(2,1)S(1)} collective-permute-done((bf16[4,32,512]{2,1,0:T(8,128)(2,1)S(1)}, bf16[4,32,512]{2,1,0:T(8,128)(2,1)S(1)}, u32[]{:S(2)}, u32[]{:S(2)}) %collective-permute-start.19) | collective-permute-done | bytes 131104 | tf_op jit(solution)/shard_map/ppermute | solution.py:20
  48.8 2.1 %collective-permute-start.6 = (bf16[288,512]{1,0:T(8,128)(2,1)S(1)}, bf16[288,512]{1,0:T(8,128)(2,1)S(1)}, u32[]{:S(2)}, u32[]{:S(2)}) collective-permute-start(bf16[288,512]{1,0:T(8,128)(2,1)S(1)} %get-tuple-element.16), channel_id=1, source_target_pairs={{0,4},{4,0},{8,12},{12,8},{16,20},{20,16},{24,28},{28,24},{1,5},{5... | collective-permute-start | bytes 884744 | tf_op jit(solution)/shard_map/ppermute | solution.py:20
  51.0 1.6 %collective-permute-start.11 = (bf16[544,512]{1,0:T(8,128)(2,1)S(1)}, bf16[544,512]{1,0:T(8,128)(2,1)S(1)}, u32[]{:S(2)}, u32[]{:S(2)}) collective-permute-start(bf16[544,512]{1,0:T(8,128)(2,1)S(1)} %get-tuple-element.15.whole), channel_id=1, source_target_pairs={{0,3},{1,2},{2,1},{3,0},{4,7},{5,6},{6,5},{7,4},{8,11},{9,10},{10,... | collective-permute-start | bytes 1671176 | tf_op jit(solution)/shard_map/ppermute | solution.py:20
  52.7 11.0 %collective-permute-done.7.refs_1_ = bf16[256,512]{1,0:T(8,128)(2,1)S(1)} collective-permute-done((bf16[256,512]{1,0:T(8,128)(2,1)S(1)}, bf16[256,512]{1,0:T(8,128)(2,1)S(1)}, u32[]{:S(2)}, u32[]{:S(2)}) %collective-permute-start.7) | collective-permute-done | bytes 262176 | tf_op jit(solution)/shard_map/ppermute | solution.py:20
  63.9 1.6 %collective-permute-start.21 = (bf16[160,512]{1,0:T(8,128)(2,1)S(1)}, bf16[160,512]{1,0:T(8,128)(2,1)S(1)}, u32[]{:S(2)}, u32[]{:S(2)}) collective-permute-start(bf16[160,512]{1,0:T(8,128)(2,1)S(1)} %fusion), channel_id=1, source_target_pairs={{0,2},{1,3},{2,0},{3,1},{4,6},{5,7},{6,4},{7,5},{8,10},{9,11},{10,... | collective-permute-start | bytes 491528 | tf_op jit(solution)/shard_map/ppermute | solution.py:20
  65.5 9.1 %collective-permute-done.9.refs_3_ = bf16[256,512]{1,0:T(8,128)(2,1)S(1)} collective-permute-done((bf16[256,512]{1,0:T(8,128)(2,1)S(1)}, bf16[256,512]{1,0:T(8,128)(2,1)S(1)}, u32[]{:S(2)}, u32[]{:S(2)}) %collective-permute-start.9) | collective-permute-done | bytes 262176 | tf_op jit(solution)/shard_map/ppermute | solution.py:20
  74.6 4.7 %collective-permute-done.8.refs_2_ = bf16[288,512]{1,0:T(8,128)(2,1)S(1)} collective-permute-done((bf16[288,512]{1,0:T(8,128)(2,1)S(1)}, bf16[288,512]{1,0:T(8,128)(2,1)S(1)}, u32[]{:S(2)}, u32[]{:S(2)}) %collective-permute-start.8) | collective-permute-done | bytes 294944 | tf_op jit(solution)/shard_map/ppermute | solution.py:20
  80.2 1.1 %shard_map.80 = bf16[512,512]{1,0:T(8,128)(2,1)} custom-call(f32[512,512]{1,0:T(8,128)S(1)} %get-tuple-element.18.total, bf16[160,512]{1,0:T(8,128)(2,1)S(1)} %get-tuple-element.19.basis, bf16[160,512]{1,0:T(8,128)(2,1)S(1)} %slice_bitcast_fusion.3.refs_0_, bf16[160,512]{1,0:T(8,128)(2,1)S(1)} %slice_bitcast_fusion.2.refs_1_, ...), custom_call_target="tpu_custom_call" | custom-call | flops 83886080 | bytes 1048576 | tf_op jit(solution)/shard_map/pallas_call | solution.py:212
  (53 shorter events, 5.3 us)
Async XLA Ops:
  0.0 6.4 %copy-start.1 = (bf16[1,1,512,512]{3,2,1,0:T(8,128)(2,1)S(1)}, bf16[1,1,512,512]{3,2,1,0:T(8,128)(2,1)}, u32[]{:S(2)}) copy-start(bf16[1,1,512,512]{3,2,1,0:T(8,128)(2,1)} %param.7) | copy-start | bytes 1572868
  1.1 10.2 %collective-permute-start = (bf16[256,512]{1,0:T(8,128)(2,1)S(1)}, bf16[256,512]{1,0:T(8,128)(2,1)S(1)}, u32[]{:S(2)}, u32[]{:S(2)}) collective-permute-start(bf16[256,512]{1,0:T(8,128)(2,1)S(1)} %get-tuple-element.24), channel_id=1, source_target_pairs={{0,4},{4,0},{8,12},{12,8},{16,20},{20,16},{24,28},{28,24},{1,5},{5... | collective-permute-start | bytes 786440 | tf_op jit(solution)/shard_map/ppermute | solution.py:20
  4.2 11.9 %collective-permute-start.1 = (bf16[256,512]{1,0:T(8,128)(2,1)S(1)}, bf16[256,512]{1,0:T(8,128)(2,1)S(1)}, u32[]{:S(2)}, u32[]{:S(2)}) collective-permute-start(bf16[256,512]{1,0:T(8,128)(2,1)S(1)} %get-tuple-element.23), channel_id=1, source_target_pairs={{0,4},{4,0},{8,12},{12,8},{16,20},{20,16},{24,28},{28,24},{1,5},{5... | collective-permute-start | bytes 786440 | tf_op jit(solution)/shard_map/ppermute | solution.py:20
  4.3 4.0 %collective-permute-start.12 = (bf16[1,128,128]{2,1,0:T(8,128)(2,1)S(1)}, bf16[1,128,128]{2,1,0:T(8,128)(2,1)S(1)}, u32[]{:S(2)}, u32[]{:S(2)}) collective-permute-start(bf16[1,128,128]{2,1,0:T(8,128)(2,1)S(1)} %shard_map.77), channel_id=1, source_target_pairs={{0,8},{4,12},{8,0},{12,4},{16,24},{20,28},{24,16},{28,20},{1,9},{5... | collective-permute-start | bytes 98312 | tf_op jit(solution)/shard_map/ppermute | solution.py:20
  6.4 19.8 %collective-permute-start.4 = (bf16[512,512]{1,0:T(8,128)(2,1)S(1)}, bf16[512,512]{1,0:T(8,128)(2,1)S(1)}, u32[]{:S(2)}, u32[]{:S(2)}) collective-permute-start(bf16[512,512]{1,0:T(8,128)(2,1)S(1)} %bitcast.18), channel_id=1, source_target_pairs={{0,1},{1,0},{2,3},{3,2},{4,5},{5,4},{6,7},{7,6},{8,9},{9,8},{10,11... | collective-permute-start | bytes 1572872 | tf_op jit(solution)/shard_map/ppermute | solution.py:20
  6.4 19.8 %collective-permute-start.5 = (bf16[512,512]{1,0:T(8,128)(2,1)S(1)}, bf16[512,512]{1,0:T(8,128)(2,1)S(1)}, u32[]{:S(2)}, u32[]{:S(2)}) collective-permute-start(bf16[512,512]{1,0:T(8,128)(2,1)S(1)} %bitcast.19), channel_id=1, source_target_pairs={{0,3},{1,2},{2,1},{3,0},{4,7},{5,6},{6,5},{7,4},{8,11},{9,10},{10,... | collective-permute-start | bytes 1572872 | tf_op jit(solution)/shard_map/ppermute | solution.py:20
  8.3 9.6 %collective-permute-start.13 = (bf16[2,128,128]{2,1,0:T(8,128)(2,1)S(1)}, bf16[2,128,128]{2,1,0:T(8,128)(2,1)S(1)}, u32[]{:S(2)}, u32[]{:S(2)}) collective-permute-start(bf16[2,128,128]{2,1,0:T(8,128)(2,1)S(1)} %pad_maximum_fusion.2), channel_id=1, source_target_pairs={{0,16},{4,20},{8,24},{12,28},{16,0},{20,4},{24,8},{28,12},{1,17},{... | collective-permute-start | bytes 196616 | tf_op jit(solution)/shard_map/ppermute | solution.py:20
  11.4 13.2 %collective-permute-start.2 = (bf16[256,512]{1,0:T(8,128)(2,1)S(1)}, bf16[256,512]{1,0:T(8,128)(2,1)S(1)}, u32[]{:S(2)}, u32[]{:S(2)}) collective-permute-start(bf16[256,512]{1,0:T(8,128)(2,1)S(1)} %collective-permute-done.refs_0_), channel_id=1, source_target_pairs={{0,8},{4,28},{8,16},{12,4},{16,24},{20,12},{24,0},{28,20},{1,9},{5... | collective-permute-start | bytes 786440 | tf_op jit(solution)/shard_map/ppermute | solution.py:20
  16.1 10.1 %collective-permute-start.3 = (bf16[256,512]{1,0:T(8,128)(2,1)S(1)}, bf16[256,512]{1,0:T(8,128)(2,1)S(1)}, u32[]{:S(2)}, u32[]{:S(2)}) collective-permute-start(bf16[256,512]{1,0:T(8,128)(2,1)S(1)} %collective-permute-done.1.refs_1_), channel_id=1, source_target_pairs={{0,8},{4,28},{8,16},{12,4},{16,24},{20,12},{24,0},{28,20},{1,9},{5... | collective-permute-start | bytes 786440 | tf_op jit(solution)/shard_map/ppermute | solution.py:20
  17.9 8.3 %copy-start.2 = (bf16[1,1,32,512]{3,2,1,0:T(8,128)(2,1)S(1)}, bf16[1,1,32,512]{3,2,1,0:T(8,128)(2,1)}, u32[]{:S(2)}) copy-start(bf16[1,1,32,512]{3,2,1,0:T(8,128)(2,1)} %param.10) | copy-start | bytes 98308
  18.0 6.5 %collective-permute-start.14 = (bf16[4,128,128]{2,1,0:T(8,128)(2,1)S(1)}, bf16[4,128,128]{2,1,0:T(8,128)(2,1)S(1)}, u32[]{:S(2)}, u32[]{:S(2)}) collective-permute-start(bf16[4,128,128]{2,1,0:T(8,128)(2,1)S(1)} %pad_maximum_fusion.1), channel_id=1, source_target_pairs={{0,4},{4,0},{8,12},{12,8},{16,20},{20,16},{24,28},{28,24},{1,5},{5... | collective-permute-start | bytes 393224 | tf_op jit(solution)/shard_map/ppermute | solution.py:20
  24.5 19.7 %collective-permute-start.15 = (bf16[8,128,128]{2,1,0:T(8,128)(2,1)S(1)}, bf16[8,128,128]{2,1,0:T(8,128)(2,1)S(1)}, u32[]{:S(2)}, u32[]{:S(2)}) collective-permute-start(bf16[8,128,128]{2,1,0:T(8,128)(2,1)S(1)} %pad_maximum_fusion.stack), channel_id=1, source_target_pairs={{0,1},{1,0},{2,3},{3,2},{4,5},{5,4},{6,7},{7,6},{8,9},{9,8},{10,11... | collective-permute-start | bytes 786440 | tf_op jit(solution)/shard_map/ppermute | solution.py:20
  28.0 8.5 %collective-permute-start.16 = (bf16[1,32,512]{2,1,0:T(8,128)(2,1)S(1)}, bf16[1,32,512]{2,1,0:T(8,128)(2,1)S(1)}, u32[]{:S(2)}, u32[]{:S(2)}) collective-permute-start(bf16[1,32,512]{2,1,0:T(8,128)(2,1)S(1)} %get-tuple-element.20), channel_id=1, source_target_pairs={{0,8},{4,12},{8,0},{12,4},{16,24},{20,28},{24,16},{28,20},{1,9},{5... | collective-permute-start | bytes 98312 | tf_op jit(solution)/shard_map/ppermute | solution.py:20
  28.1 11.0 %collective-permute-start.17 = (bf16[1,32,512]{2,1,0:T(8,128)(2,1)S(1)}, bf16[1,32,512]{2,1,0:T(8,128)(2,1)S(1)}, u32[]{:S(2)}, u32[]{:S(2)}) collective-permute-start(bf16[1,32,512]{2,1,0:T(8,128)(2,1)S(1)} %get-tuple-element.20), channel_id=1, source_target_pairs={{0,16},{4,20},{8,24},{12,28},{16,0},{20,4},{24,8},{28,12},{1,17},{... | collective-permute-start | bytes 98312 | tf_op jit(solution)/shard_map/ppermute | solution.py:20
  36.5 5.7 %collective-permute-start.18 = (bf16[1,32,512]{2,1,0:T(8,128)(2,1)S(1)}, bf16[1,32,512]{2,1,0:T(8,128)(2,1)S(1)}, u32[]{:S(2)}, u32[]{:S(2)}) collective-permute-start(bf16[1,32,512]{2,1,0:T(8,128)(2,1)S(1)} %get-tuple-element.20), channel_id=1, source_target_pairs={{0,24},{4,28},{8,16},{12,20},{16,8},{20,12},{24,0},{28,4},{1,25},{... | collective-permute-start | bytes 98312 | tf_op jit(solution)/shard_map/ppermute | solution.py:20
  42.2 5.0 %collective-permute-start.19 = (bf16[4,32,512]{2,1,0:T(8,128)(2,1)S(1)}, bf16[4,32,512]{2,1,0:T(8,128)(2,1)S(1)}, u32[]{:S(2)}, u32[]{:S(2)}) collective-permute-start(bf16[4,32,512]{2,1,0:T(8,128)(2,1)S(1)} %constant_dynamic-update-slice_fusion.refs_0_), channel_id=1, source_target_pairs={{0,4},{4,0},{8,12},{12,8},{16,20},{20,16},{24,28},{28,24},{1,5},{5... | collective-permute-start | bytes 393224 | tf_op jit(solution)/shard_map/ppermute | solution.py:20
  47.5 16.4 %collective-permute-start.20 = (bf16[2,160,512]{2,1,0:T(8,128)(2,1)S(1)}, bf16[2,160,512]{2,1,0:T(8,128)(2,1)S(1)}, u32[]{:S(2)}, u32[]{:S(2)}) collective-permute-start(bf16[2,160,512]{2,1,0:T(8,128)(2,1)S(1)} %get-tuple-element.22), channel_id=1, source_target_pairs={{0,1},{1,0},{2,3},{3,2},{4,5},{5,4},{6,7},{7,6},{8,9},{9,8},{10,11... | collective-permute-start | bytes 983048 | tf_op jit(solution)/shard_map/ppermute | solution.py:20
  48.8 14.8 %collective-permute-start.6 = (bf16[288,512]{1,0:T(8,128)(2,1)S(1)}, bf16[288,512]{1,0:T(8,128)(2,1)S(1)}, u32[]{:S(2)}, u32[]{:S(2)}) collective-permute-start(bf16[288,512]{1,0:T(8,128)(2,1)S(1)} %get-tuple-element.16), channel_id=1, source_target_pairs={{0,4},{4,0},{8,12},{12,8},{16,20},{20,16},{24,28},{28,24},{1,5},{5... | collective-permute-start | bytes 884744 | tf_op jit(solution)/shard_map/ppermute | solution.py:20
  50.9 12.7 %collective-permute-start.7 = (bf16[256,512]{1,0:T(8,128)(2,1)S(1)}, bf16[256,512]{1,0:T(8,128)(2,1)S(1)}, u32[]{:S(2)}, u32[]{:S(2)}) collective-permute-start(bf16[256,512]{1,0:T(8,128)(2,1)S(1)} %get-tuple-element.17), channel_id=1, source_target_pairs={{0,4},{4,0},{8,12},{12,8},{16,20},{20,16},{24,28},{28,24},{1,5},{5... | collective-permute-start | bytes 786440 | tf_op jit(solution)/shard_map/ppermute | solution.py:20
  51.0 23.6 %collective-permute-start.10 = (bf16[544,512]{1,0:T(8,128)(2,1)S(1)}, bf16[544,512]{1,0:T(8,128)(2,1)S(1)}, u32[]{:S(2)}, u32[]{:S(2)}) collective-permute-start(bf16[544,512]{1,0:T(8,128)(2,1)S(1)} %get-tuple-element.15.whole), channel_id=1, source_target_pairs={{0,1},{1,0},{2,3},{3,2},{4,5},{5,4},{6,7},{7,6},{8,9},{9,8},{10,11... | collective-permute-start | bytes 1671176 | tf_op jit(solution)/shard_map/ppermute | solution.py:20
  51.0 23.6 %collective-permute-start.11 = (bf16[544,512]{1,0:T(8,128)(2,1)S(1)}, bf16[544,512]{1,0:T(8,128)(2,1)S(1)}, u32[]{:S(2)}, u32[]{:S(2)}) collective-permute-start(bf16[544,512]{1,0:T(8,128)(2,1)S(1)} %get-tuple-element.15.whole), channel_id=1, source_target_pairs={{0,3},{1,2},{2,1},{3,0},{4,7},{5,6},{6,5},{7,4},{8,11},{9,10},{10,... | collective-permute-start | bytes 1671176 | tf_op jit(solution)/shard_map/ppermute | solution.py:20
  63.6 11.0 %collective-permute-start.9 = (bf16[256,512]{1,0:T(8,128)(2,1)S(1)}, bf16[256,512]{1,0:T(8,128)(2,1)S(1)}, u32[]{:S(2)}, u32[]{:S(2)}) collective-permute-start(bf16[256,512]{1,0:T(8,128)(2,1)S(1)} %collective-permute-done.7.refs_1_), channel_id=1, source_target_pairs={{0,8},{4,28},{8,16},{12,4},{16,24},{20,12},{24,0},{28,20},{1,9},{5... | collective-permute-start | bytes 786440 | tf_op jit(solution)/shard_map/ppermute | solution.py:20
  63.6 15.7 %collective-permute-start.8 = (bf16[288,512]{1,0:T(8,128)(2,1)S(1)}, bf16[288,512]{1,0:T(8,128)(2,1)S(1)}, u32[]{:S(2)}, u32[]{:S(2)}) collective-permute-start(bf16[288,512]{1,0:T(8,128)(2,1)S(1)} %collective-permute-done.6.refs_0_), channel_id=1, source_target_pairs={{0,8},{4,28},{8,16},{12,4},{16,24},{20,12},{24,0},{28,20},{1,9},{5... | collective-permute-start | bytes 884744 | tf_op jit(solution)/shard_map/ppermute | solution.py:20
  63.9 16.3 %collective-permute-start.21 = (bf16[160,512]{1,0:T(8,128)(2,1)S(1)}, bf16[160,512]{1,0:T(8,128)(2,1)S(1)}, u32[]{:S(2)}, u32[]{:S(2)}) collective-permute-start(bf16[160,512]{1,0:T(8,128)(2,1)S(1)} %fusion), channel_id=1, source_target_pairs={{0,2},{1,3},{2,0},{3,1},{4,6},{5,7},{6,4},{7,5},{8,10},{9,11},{10,... | collective-permute-start | bytes 491528 | tf_op jit(solution)/shard_map/ppermute | solution.py:20
  (5 other events, 11.5 us)

commit v3 on v2

--- a/solution.py
+++ b/solution.py
@@ -10,7 +10,6 @@
 
 MOST_WEIGHTS = 1 << 20
 CUTS_ONE = (4,)
-CUTS_TWO = (4,)
 VMEM = pl.BlockSpec(memory_space=pltpu.VMEM)
 SMEM = pl.BlockSpec(memory_space=pltpu.SMEM)
 
@@ -125,24 +124,23 @@
     )
 
 
-def join_kernel(blocks, counts, codes, own, defl, *refs):
-    *pieces, shared, restricted = refs
-    width = own.shape[1] // blocks
-    fields = [[pieces.pop(0) for _ in range(count)] for count in counts]
+def join_kernel(blocks, low, codes, own, defl, near_g, far_g, near_m, far_m, *refs):
+    *before, shared, restricted = refs
+    size, columns = shared.shape
+    width = columns // blocks
+    rows = slice(low, low + size)
     for n in range(blocks):
         cols = slice(n * width, (n + 1) * width)
-        for code, field in enumerate(fields):
+        for code, (ref, place) in enumerate(((near_g, slice(0, size)), (far_g, slice(0, size)), (near_m, rows), (far_m, rows))):
 
             @pl.when(chosen(codes, n) == code)
             def _():
-                row = 0
-                for ref in field:
-                    place = slice(row, row + ref.shape[0])
-                    total = own[place, cols].astype(jnp.float32) + ref[:, cols].astype(jnp.float32)
-                    shared[place, cols] = total.astype(jnp.bfloat16)
-                    row += ref.shape[0]
-
-    restricted[0] = lax.dot_general(
+                total = own[rows, cols].astype(jnp.float32) + ref[place, cols].astype(jnp.float32)
+                shared[:, cols] = total.astype(jnp.bfloat16)
+
+    for ref in before:
+        restricted[0, :, :low] = ref[0]
+    restricted[0, :, rows] = lax.dot_general(
         defl[...], shared[...], (((1,), (1,)), ((), ())), preferred_element_type=jnp.float32
     ).astype(jnp.bfloat16)
 
@@ -152,18 +150,20 @@
     basis[...] = (defl[...].astype(jnp.float32) - scale[...] * defl_schur).astype(jnp.bfloat16)
 
 
-def base_kernel(shared, basis, schur, scale, whole, *chunks):
-    vectors = basis.shape[0]
+def base_kernel(shared, basis, schur, scale, *refs):
+    *before, chunk = refs[:-1] if len(refs) > 1 else refs
     base = jnp.dot(shared[...], schur[...], preferred_element_type=jnp.float32)
     base = (scale[...] * base).astype(jnp.bfloat16)
-    whole[:vectors] = basis[...]
-    whole[vectors:] = base
-    chunks[0][:vectors] = basis[...]
-    row = -vectors
-    for chunk in chunks:
-        skip = max(-row, 0)
-        chunk[skip:] = base[row + skip : row + chunk.shape[0]]
-        row += chunk.shape[0]
+    skip = chunk.shape[0] - base.shape[0]
+    if skip:
+        chunk[:skip] = basis[...]
+    chunk[skip:] = base
+    if before:
+        whole, row = refs[-1], 0
+        for ref in before:
+            whole[row : row + ref.shape[0]] = ref[...]
+            row += ref.shape[0]
+        whole[row:] = base
 
 
 def solve_kernel(weights, *refs):
@@ -272,14 +272,6 @@
     if gathered:
         weights = coarse_weights(forward_panels, block_inverses, vectors)
 
-    shared, restricted = call(
-        functools.partial(join_kernel, blocks, (len(near_g), len(far_g), 1, 1)),
-        [bf16((rows, columns)), bf16((1, vectors, rows))],
-        [SMEM] + [VMEM] * (4 + len(near_g) + len(far_g)),
-        [],
-        2 * rows * columns * vectors,
-        codes, field, defl, *near_g, *far_g, near_m, far_m,
-    )
     basis = call(
         basis_kernel,
         bf16((vectors, columns)),
@@ -288,16 +280,29 @@
         2 * vectors * columns * columns,
         defl, local_schur, scale,
     )
-    sizes = chunk_sizes(rows, CUTS_TWO)
-    sizes[0] += vectors
-    whole, *chunks = call(
-        base_kernel,
-        [bf16((vectors + rows, columns))] + [bf16((size, columns)) for size in sizes],
-        [VMEM] * 4,
-        [],
-        2 * rows * columns * columns,
-        shared, basis, local_schur, scale,
-    )
+    low, before, chunks = 0, [], []
+    sizes = chunk_sizes(rows, CUTS_ONE)
+    for i, size in enumerate(sizes):
+        shared, restricted = call(
+            functools.partial(join_kernel, blocks, low),
+            [bf16((size, columns)), bf16((1, vectors, low + size))],
+            [SMEM] + [VMEM] * (6 + len(before)),
+            [],
+            2 * size * columns * vectors,
+            codes, field, defl, near_g[i], far_g[i], near_m, far_m, *before,
+        )
+        last = i == len(sizes) - 1
+        shapes = [bf16((size + (0 if i else vectors), columns))] + [bf16((vectors + rows, columns))] * last
+        chunk, *whole = call(
+            base_kernel,
+            shapes,
+            [VMEM] * (4 + len(chunks) * last),
+            [],
+            2 * size * columns * columns,
+            shared, basis, local_schur, scale, *(chunks if last else []),
+        )
+        low, before, chunks = low + size, [restricted], [*chunks, chunk]
+    whole = whole[0]
     two_near_g = [swap(chunk, "grp", near) for chunk in chunks]
     two_far_g = [swap(chunk, "grp", onward(groups)) for chunk in two_near_g]
     two_near_m = swap(whole, "sub", near)

time: 81.5 us -> 82.2 us (level)
  Pallas kernels: 5.92 us -> 6.92 us
    pallas_call x8 -> x10, Pallas kernels: 5.92 us -> 6.92 us  [call(): pl.pallas_call(kernel, out_shape=shapes, in_specs=in_specs, out_specs=VME...]
  transfers between devices with their start and end apart: 22 -> 22, of which waited for: 10 -> 10; matrix products, arithmetic and copies ran while one was open for 0% -> 0% of each run, Pallas kernels for 5% -> 7%
where the time goes in v3:
time: 82.2 us; the launch traced here: 82.1 us
  waiting for transfers between devices  38.7 us (47%)
  starting transfers between devices  33.7 us (41%)
  Pallas kernels  6.92 us (8%)
  local copies, waits for them, and re-layouts  2.42 us (3%)
    ppermute x22, waiting for transfers between devices, swap(): return lax.ppermute(block, axis, route)  38.7 us
    ppermute x22, starting transfers between devices, swap(): return lax.ppermute(block, axis, route)  33.7 us
    pallas_call x10, Pallas kernels, call(): pl.pallas_call(kernel, out_shape=shapes, in_specs=in_specs, out_specs=VME...  6.92 us
  transfers between devices with their start and end apart: 22, of which 10 were waited for; matrix products, arithmetic and copies ran while one was open for 0% of the time, Pallas kernels for 7%

profile of v3, /device:TPU:0, one launch (start us, length us, event | category | flops | bytes accessed | tf_op | source)
XLA Modules:
  0.0 82.1 jit_solution(1358314438161943198)
XLA Ops:
  0.0 1.1 %slice_bitcast_fusion = (bf16[256,512]{1,0:T(8,128)(2,1)S(1)}, bf16[256,512]{1,0:T(8,128)(2,1)S(1)}) fusion(bf16[1,1,512,512]{3,2,1,0:T(8,128)(2,1)} %param.7), kind=kLoop, calls=%fused_computation.2 | loop fusion | bytes 1048576 | tf_op jit(solution)/shard_map/slice | solution.py:265
  1.1 3.0 %collective-permute-start = (bf16[256,512]{1,0:T(8,128)(2,1)S(1)}, bf16[256,512]{1,0:T(8,128)(2,1)S(1)}, u32[]{:S(2)}, u32[]{:S(2)}) collective-permute-start(bf16[256,512]{1,0:T(8,128)(2,1)S(1)} %get-tuple-element.26), channel_id=1, source_target_pairs={{0,4},{4,0},{8,12},{12,8},{16,20},{20,16},{24,28},{28,24},{1,5},{5... | collective-permute-start | bytes 786440 | tf_op jit(solution)/shard_map/ppermute | solution.py:19
  4.3 2.1 %collective-permute-start.12 = (bf16[1,128,128]{2,1,0:T(8,128)(2,1)S(1)}, bf16[1,128,128]{2,1,0:T(8,128)(2,1)S(1)}, u32[]{:S(2)}, u32[]{:S(2)}) collective-permute-start(bf16[1,128,128]{2,1,0:T(8,128)(2,1)S(1)} %shard_map.79), channel_id=1, source_target_pairs={{0,8},{4,12},{8,0},{12,4},{16,24},{20,28},{24,16},{28,20},{1,9},{5... | collective-permute-start | bytes 98312 | tf_op jit(solution)/shard_map/ppermute | solution.py:19
  6.4 1.6 %collective-permute-start.3 = (bf16[512,512]{1,0:T(8,128)(2,1)S(1)}, bf16[512,512]{1,0:T(8,128)(2,1)S(1)}, u32[]{:S(2)}, u32[]{:S(2)}) collective-permute-start(bf16[512,512]{1,0:T(8,128)(2,1)S(1)} %bitcast.17), channel_id=1, source_target_pairs={{0,3},{1,2},{2,1},{3,0},{4,7},{5,6},{6,5},{7,4},{8,11},{9,10},{10,... | collective-permute-start | bytes 1572872 | tf_op jit(solution)/shard_map/ppermute | solution.py:19
  8.3 3.1 %collective-permute-start.13 = (bf16[2,128,128]{2,1,0:T(8,128)(2,1)S(1)}, bf16[2,128,128]{2,1,0:T(8,128)(2,1)S(1)}, u32[]{:S(2)}, u32[]{:S(2)}) collective-permute-start(bf16[2,128,128]{2,1,0:T(8,128)(2,1)S(1)} %pad_maximum_fusion.2), channel_id=1, source_target_pairs={{0,16},{4,20},{8,24},{12,28},{16,0},{20,4},{24,8},{28,12},{1,17},{... | collective-permute-start | bytes 196616 | tf_op jit(solution)/shard_map/ppermute | solution.py:19
  11.4 2.1 %collective-permute-start.1 = (bf16[256,512]{1,0:T(8,128)(2,1)S(1)}, bf16[256,512]{1,0:T(8,128)(2,1)S(1)}, u32[]{:S(2)}, u32[]{:S(2)}) collective-permute-start(bf16[256,512]{1,0:T(8,128)(2,1)S(1)} %collective-permute-done.near_g), channel_id=1, source_target_pairs={{0,8},{4,28},{8,16},{12,4},{16,24},{20,12},{24,0},{28,20},{1,9},{5... | collective-permute-start | bytes 786440 | tf_op jit(solution)/shard_map/ppermute | solution.py:19
  13.4 2.7 %collective-permute-done.4.near_g = bf16[256,512]{1,0:T(8,128)(2,1)S(1)} collective-permute-done((bf16[256,512]{1,0:T(8,128)(2,1)S(1)}, bf16[256,512]{1,0:T(8,128)(2,1)S(1)}, u32[]{:S(2)}, u32[]{:S(2)}) %collective-permute-start.4) | collective-permute-done | bytes 262176 | tf_op jit(solution)/shard_map/ppermute | solution.py:19
  16.1 1.8 %collective-permute-start.5 = (bf16[256,512]{1,0:T(8,128)(2,1)S(1)}, bf16[256,512]{1,0:T(8,128)(2,1)S(1)}, u32[]{:S(2)}, u32[]{:S(2)}) collective-permute-start(bf16[256,512]{1,0:T(8,128)(2,1)S(1)} %collective-permute-done.4.near_g), channel_id=1, source_target_pairs={{0,8},{4,28},{8,16},{12,4},{16,24},{20,12},{24,0},{28,20},{1,9},{5... | collective-permute-start | bytes 786440 | tf_op jit(solution)/shard_map/ppermute | solution.py:19
  18.0 3.6 %collective-permute-start.14 = (bf16[4,128,128]{2,1,0:T(8,128)(2,1)S(1)}, bf16[4,128,128]{2,1,0:T(8,128)(2,1)S(1)}, u32[]{:S(2)}, u32[]{:S(2)}) collective-permute-start(bf16[4,128,128]{2,1,0:T(8,128)(2,1)S(1)} %pad_maximum_fusion.1), channel_id=1, source_target_pairs={{0,4},{4,0},{8,12},{12,8},{16,20},{20,16},{24,28},{28,24},{1,5},{5... | collective-permute-start | bytes 393224 | tf_op jit(solution)/shard_map/ppermute | solution.py:19
  21.5 2.9 %collective-permute-done.14 = bf16[4,128,128]{2,1,0:T(8,128)(2,1)S(1)} collective-permute-done((bf16[4,128,128]{2,1,0:T(8,128)(2,1)S(1)}, bf16[4,128,128]{2,1,0:T(8,128)(2,1)S(1)}, u32[]{:S(2)}, u32[]{:S(2)}) %collective-permute-start.14) | collective-permute-done | bytes 131104 | tf_op jit(solution)/shard_map/ppermute | solution.py:19
  24.6 1.6 %collective-permute-done.5.far_g = bf16[256,512]{1,0:T(8,128)(2,1)S(1)} collective-permute-done((bf16[256,512]{1,0:T(8,128)(2,1)S(1)}, bf16[256,512]{1,0:T(8,128)(2,1)S(1)}, u32[]{:S(2)}, u32[]{:S(2)}) %collective-permute-start.5) | collective-permute-done | bytes 262176 | tf_op jit(solution)/shard_map/ppermute | solution.py:19
  28.9 8.4 %collective-permute-start.17 = (bf16[1,32,512]{2,1,0:T(8,128)(2,1)S(1)}, bf16[1,32,512]{2,1,0:T(8,128)(2,1)S(1)}, u32[]{:S(2)}, u32[]{:S(2)}) collective-permute-start(bf16[1,32,512]{2,1,0:T(8,128)(2,1)S(1)} %get-tuple-element.22), channel_id=1, source_target_pairs={{0,16},{4,20},{8,24},{12,28},{16,0},{20,4},{24,8},{28,12},{1,17},{... | collective-permute-start | bytes 98312 | tf_op jit(solution)/shard_map/ppermute | solution.py:19
  37.4 2.6 %collective-permute-done.17 = bf16[1,32,512]{2,1,0:T(8,128)(2,1)S(1)} collective-permute-done((bf16[1,32,512]{2,1,0:T(8,128)(2,1)S(1)}, bf16[1,32,512]{2,1,0:T(8,128)(2,1)S(1)}, u32[]{:S(2)}, u32[]{:S(2)}) %collective-permute-start.17) | collective-permute-done | bytes 32800 | tf_op jit(solution)/shard_map/ppermute | solution.py:19
  39.9 3.1 %collective-permute-done.18 = bf16[1,32,512]{2,1,0:T(8,128)(2,1)S(1)} collective-permute-done((bf16[1,32,512]{2,1,0:T(8,128)(2,1)S(1)}, bf16[1,32,512]{2,1,0:T(8,128)(2,1)S(1)}, u32[]{:S(2)}, u32[]{:S(2)}) %collective-permute-start.18) | collective-permute-done | bytes 32800 | tf_op jit(solution)/shard_map/ppermute | solution.py:19
  43.1 2.0 %collective-permute-start.19 = (bf16[4,32,512]{2,1,0:T(8,128)(2,1)S(1)}, bf16[4,32,512]{2,1,0:T(8,128)(2,1)S(1)}, u32[]{:S(2)}, u32[]{:S(2)}) collective-permute-start(bf16[4,32,512]{2,1,0:T(8,128)(2,1)S(1)} %constant_dynamic-update-slice_fusion.refs_0_), channel_id=1, source_target_pairs={{0,4},{4,0},{8,12},{12,8},{16,20},{20,16},{24,28},{28,24},{1,5},{5... | collective-permute-start | bytes 393224 | tf_op jit(solution)/shard_map/ppermute | solution.py:19
  45.1 1.7 %shard_map.80.weights = bf16[4,160,256]{2,1,0:T(8,128)(2,1)S(1)} custom-call(bf16[8,128,128]{2,1,0:T(8,128)(2,1)S(1)} %pad_maximum_fusion.stack, bf16[8,128,128]{2,1,0:T(8,128)(2,1)S(1)} %collective-permute-done.15.other), custom_call_target="tpu_custom_call" | custom-call | flops 201326592 | bytes 1048576 | tf_op jit(solution)/shard_map/pallas_call | solution.py:212
  46.8 1.2 %collective-permute-done.19.refs_1_ = bf16[4,32,512]{2,1,0:T(8,128)(2,1)S(1)} collective-permute-done((bf16[4,32,512]{2,1,0:T(8,128)(2,1)S(1)}, bf16[4,32,512]{2,1,0:T(8,128)(2,1)S(1)}, u32[]{:S(2)}, u32[]{:S(2)}) %collective-permute-start.19) | collective-permute-done | bytes 131104 | tf_op jit(solution)/shard_map/ppermute | solution.py:19
  49.6 2.1 %collective-permute-start.6 = (bf16[288,512]{1,0:T(8,128)(2,1)S(1)}, bf16[288,512]{1,0:T(8,128)(2,1)S(1)}, u32[]{:S(2)}, u32[]{:S(2)}) collective-permute-start(bf16[288,512]{1,0:T(8,128)(2,1)S(1)} %shard_map.76.refs_0_), channel_id=1, source_target_pairs={{0,4},{4,0},{8,12},{12,8},{16,20},{20,16},{24,28},{28,24},{1,5},{5... | collective-permute-start | bytes 884744 | tf_op jit(solution)/shard_map/ppermute | solution.py:19
  52.1 1.6 %collective-permute-start.11 = (bf16[544,512]{1,0:T(8,128)(2,1)S(1)}, bf16[544,512]{1,0:T(8,128)(2,1)S(1)}, u32[]{:S(2)}, u32[]{:S(2)}) collective-permute-start(bf16[544,512]{1,0:T(8,128)(2,1)S(1)} %get-tuple-element.18.whole), channel_id=1, source_target_pairs={{0,3},{1,2},{2,1},{3,0},{4,7},{5,6},{6,5},{7,4},{8,11},{9,10},{10,... | collective-permute-start | bytes 1671176 | tf_op jit(solution)/shard_map/ppermute | solution.py:19
  53.7 10.6 %collective-permute-done.7.refs_1_ = bf16[256,512]{1,0:T(8,128)(2,1)S(1)} collective-permute-done((bf16[256,512]{1,0:T(8,128)(2,1)S(1)}, bf16[256,512]{1,0:T(8,128)(2,1)S(1)}, u32[]{:S(2)}, u32[]{:S(2)}) %collective-permute-start.7) | collective-permute-done | bytes 262176 | tf_op jit(solution)/shard_map/ppermute | solution.py:19
  64.7 1.6 %collective-permute-start.21 = (bf16[160,512]{1,0:T(8,128)(2,1)S(1)}, bf16[160,512]{1,0:T(8,128)(2,1)S(1)}, u32[]{:S(2)}, u32[]{:S(2)}) collective-permute-start(bf16[160,512]{1,0:T(8,128)(2,1)S(1)} %fusion), channel_id=1, source_target_pairs={{0,2},{1,3},{2,0},{3,1},{4,6},{5,7},{6,4},{7,5},{8,10},{9,11},{10,... | collective-permute-start | bytes 491528 | tf_op jit(solution)/shard_map/ppermute | solution.py:19
  66.2 9.1 %collective-permute-done.9.refs_3_ = bf16[256,512]{1,0:T(8,128)(2,1)S(1)} collective-permute-done((bf16[256,512]{1,0:T(8,128)(2,1)S(1)}, bf16[256,512]{1,0:T(8,128)(2,1)S(1)}, u32[]{:S(2)}, u32[]{:S(2)}) %collective-permute-start.9) | collective-permute-done | bytes 262176 | tf_op jit(solution)/shard_map/ppermute | solution.py:19
  75.3 4.7 %collective-permute-done.8.refs_2_ = bf16[288,512]{1,0:T(8,128)(2,1)S(1)} collective-permute-done((bf16[288,512]{1,0:T(8,128)(2,1)S(1)}, bf16[288,512]{1,0:T(8,128)(2,1)S(1)}, u32[]{:S(2)}, u32[]{:S(2)}) %collective-permute-start.8) | collective-permute-done | bytes 294944 | tf_op jit(solution)/shard_map/ppermute | solution.py:19
  80.9 1.1 %shard_map.82 = bf16[512,512]{1,0:T(8,128)(2,1)} custom-call(f32[512,512]{1,0:T(8,128)S(1)} %get-tuple-element.20.total, bf16[160,512]{1,0:T(8,128)(2,1)S(1)} %get-tuple-element.21.basis, bf16[160,512]{1,0:T(8,128)(2,1)S(1)} %slice_bitcast_fusion.3.refs_0_, bf16[160,512]{1,0:T(8,128)(2,1)S(1)} %slice_bitcast_fusion.2.refs_1_, ...), custom_call_target="tpu_custom_call" | custom-call | flops 83886080 | bytes 1048576 | tf_op jit(solution)/shard_map/pallas_call | solution.py:212
  (55 shorter events, 6.4 us)
Async XLA Ops:
  0.0 6.4 %copy-start = (bf16[1,1,512,512]{3,2,1,0:T(8,128)(2,1)S(1)}, bf16[1,1,512,512]{3,2,1,0:T(8,128)(2,1)}, u32[]{:S(2)}) copy-start(bf16[1,1,512,512]{3,2,1,0:T(8,128)(2,1)} %param.7) | copy-start | bytes 1572868
  1.1 10.2 %collective-permute-start = (bf16[256,512]{1,0:T(8,128)(2,1)S(1)}, bf16[256,512]{1,0:T(8,128)(2,1)S(1)}, u32[]{:S(2)}, u32[]{:S(2)}) collective-permute-start(bf16[256,512]{1,0:T(8,128)(2,1)S(1)} %get-tuple-element.26), channel_id=1, source_target_pairs={{0,4},{4,0},{8,12},{12,8},{16,20},{20,16},{24,28},{28,24},{1,5},{5... | collective-permute-start | bytes 786440 | tf_op jit(solution)/shard_map/ppermute | solution.py:19
  4.2 11.9 %collective-permute-start.4 = (bf16[256,512]{1,0:T(8,128)(2,1)S(1)}, bf16[256,512]{1,0:T(8,128)(2,1)S(1)}, u32[]{:S(2)}, u32[]{:S(2)}) collective-permute-start(bf16[256,512]{1,0:T(8,128)(2,1)S(1)} %get-tuple-element.25), channel_id=1, source_target_pairs={{0,4},{4,0},{8,12},{12,8},{16,20},{20,16},{24,28},{28,24},{1,5},{5... | collective-permute-start | bytes 786440 | tf_op jit(solution)/shard_map/ppermute | solution.py:19
  4.3 4.0 %collective-permute-start.12 = (bf16[1,128,128]{2,1,0:T(8,128)(2,1)S(1)}, bf16[1,128,128]{2,1,0:T(8,128)(2,1)S(1)}, u32[]{:S(2)}, u32[]{:S(2)}) collective-permute-start(bf16[1,128,128]{2,1,0:T(8,128)(2,1)S(1)} %shard_map.79), channel_id=1, source_target_pairs={{0,8},{4,12},{8,0},{12,4},{16,24},{20,28},{24,16},{28,20},{1,9},{5... | collective-permute-start | bytes 98312 | tf_op jit(solution)/shard_map/ppermute | solution.py:19
  6.4 18.2 %collective-permute-start.2 = (bf16[512,512]{1,0:T(8,128)(2,1)S(1)}, bf16[512,512]{1,0:T(8,128)(2,1)S(1)}, u32[]{:S(2)}, u32[]{:S(2)}) collective-permute-start(bf16[512,512]{1,0:T(8,128)(2,1)S(1)} %bitcast.16), channel_id=1, source_target_pairs={{0,1},{1,0},{2,3},{3,2},{4,5},{5,4},{6,7},{7,6},{8,9},{9,8},{10,11... | collective-permute-start | bytes 1572872 | tf_op jit(solution)/shard_map/ppermute | solution.py:19
  6.4 18.2 %collective-permute-start.3 = (bf16[512,512]{1,0:T(8,128)(2,1)S(1)}, bf16[512,512]{1,0:T(8,128)(2,1)S(1)}, u32[]{:S(2)}, u32[]{:S(2)}) collective-permute-start(bf16[512,512]{1,0:T(8,128)(2,1)S(1)} %bitcast.17), channel_id=1, source_target_pairs={{0,3},{1,2},{2,1},{3,0},{4,7},{5,6},{6,5},{7,4},{8,11},{9,10},{10,... | collective-permute-start | bytes 1572872 | tf_op jit(solution)/shard_map/ppermute | solution.py:19
  8.3 9.6 %collective-permute-start.13 = (bf16[2,128,128]{2,1,0:T(8,128)(2,1)S(1)}, bf16[2,128,128]{2,1,0:T(8,128)(2,1)S(1)}, u32[]{:S(2)}, u32[]{:S(2)}) collective-permute-start(bf16[2,128,128]{2,1,0:T(8,128)(2,1)S(1)} %pad_maximum_fusion.2), channel_id=1, source_target_pairs={{0,16},{4,20},{8,24},{12,28},{16,0},{20,4},{24,8},{28,12},{1,17},{... | collective-permute-start | bytes 196616 | tf_op jit(solution)/shard_map/ppermute | solution.py:19
  11.4 16.5 %collective-permute-start.1 = (bf16[256,512]{1,0:T(8,128)(2,1)S(1)}, bf16[256,512]{1,0:T(8,128)(2,1)S(1)}, u32[]{:S(2)}, u32[]{:S(2)}) collective-permute-start(bf16[256,512]{1,0:T(8,128)(2,1)S(1)} %collective-permute-done.near_g), channel_id=1, source_target_pairs={{0,8},{4,28},{8,16},{12,4},{16,24},{20,12},{24,0},{28,20},{1,9},{5... | collective-permute-start | bytes 786440 | tf_op jit(solution)/shard_map/ppermute | solution.py:19
  16.1 10.1 %collective-permute-start.5 = (bf16[256,512]{1,0:T(8,128)(2,1)S(1)}, bf16[256,512]{1,0:T(8,128)(2,1)S(1)}, u32[]{:S(2)}, u32[]{:S(2)}) collective-permute-start(bf16[256,512]{1,0:T(8,128)(2,1)S(1)} %collective-permute-done.4.near_g), channel_id=1, source_target_pairs={{0,8},{4,28},{8,16},{12,4},{16,24},{20,12},{24,0},{28,20},{1,9},{5... | collective-permute-start | bytes 786440 | tf_op jit(solution)/shard_map/ppermute | solution.py:19
  17.9 8.3 %copy-start.2 = (bf16[1,1,32,512]{3,2,1,0:T(8,128)(2,1)S(1)}, bf16[1,1,32,512]{3,2,1,0:T(8,128)(2,1)}, u32[]{:S(2)}) copy-start(bf16[1,1,32,512]{3,2,1,0:T(8,128)(2,1)} %param.10) | copy-start | bytes 98308
  18.0 6.5 %collective-permute-start.14 = (bf16[4,128,128]{2,1,0:T(8,128)(2,1)S(1)}, bf16[4,128,128]{2,1,0:T(8,128)(2,1)S(1)}, u32[]{:S(2)}, u32[]{:S(2)}) collective-permute-start(bf16[4,128,128]{2,1,0:T(8,128)(2,1)S(1)} %pad_maximum_fusion.1), channel_id=1, source_target_pairs={{0,4},{4,0},{8,12},{12,8},{16,20},{20,16},{24,28},{28,24},{1,5},{5... | collective-permute-start | bytes 393224 | tf_op jit(solution)/shard_map/ppermute | solution.py:19
  24.5 20.6 %collective-permute-start.15 = (bf16[8,128,128]{2,1,0:T(8,128)(2,1)S(1)}, bf16[8,128,128]{2,1,0:T(8,128)(2,1)S(1)}, u32[]{:S(2)}, u32[]{:S(2)}) collective-permute-start(bf16[8,128,128]{2,1,0:T(8,128)(2,1)S(1)} %pad_maximum_fusion.stack), channel_id=1, source_target_pairs={{0,1},{1,0},{2,3},{3,2},{4,5},{5,4},{6,7},{7,6},{8,9},{9,8},{10,11... | collective-permute-start | bytes 786440 | tf_op jit(solution)/shard_map/ppermute | solution.py:19
  28.9 8.5 %collective-permute-start.16 = (bf16[1,32,512]{2,1,0:T(8,128)(2,1)S(1)}, bf16[1,32,512]{2,1,0:T(8,128)(2,1)S(1)}, u32[]{:S(2)}, u32[]{:S(2)}) collective-permute-start(bf16[1,32,512]{2,1,0:T(8,128)(2,1)S(1)} %get-tuple-element.22), channel_id=1, source_target_pairs={{0,8},{4,12},{8,0},{12,4},{16,24},{20,28},{24,16},{28,20},{1,9},{5... | collective-permute-start | bytes 98312 | tf_op jit(solution)/shard_map/ppermute | solution.py:19
  28.9 11.0 %collective-permute-start.17 = (bf16[1,32,512]{2,1,0:T(8,128)(2,1)S(1)}, bf16[1,32,512]{2,1,0:T(8,128)(2,1)S(1)}, u32[]{:S(2)}, u32[]{:S(2)}) collective-permute-start(bf16[1,32,512]{2,1,0:T(8,128)(2,1)S(1)} %get-tuple-element.22), channel_id=1, source_target_pairs={{0,16},{4,20},{8,24},{12,28},{16,0},{20,4},{24,8},{28,12},{1,17},{... | collective-permute-start | bytes 98312 | tf_op jit(solution)/shard_map/ppermute | solution.py:19
  37.3 5.7 %collective-permute-start.18 = (bf16[1,32,512]{2,1,0:T(8,128)(2,1)S(1)}, bf16[1,32,512]{2,1,0:T(8,128)(2,1)S(1)}, u32[]{:S(2)}, u32[]{:S(2)}) collective-permute-start(bf16[1,32,512]{2,1,0:T(8,128)(2,1)S(1)} %get-tuple-element.22), channel_id=1, source_target_pairs={{0,24},{4,28},{8,16},{12,20},{16,8},{20,12},{24,0},{28,4},{1,25},{... | collective-permute-start | bytes 98312 | tf_op jit(solution)/shard_map/ppermute | solution.py:19
  43.1 5.0 %collective-permute-start.19 = (bf16[4,32,512]{2,1,0:T(8,128)(2,1)S(1)}, bf16[4,32,512]{2,1,0:T(8,128)(2,1)S(1)}, u32[]{:S(2)}, u32[]{:S(2)}) collective-permute-start(bf16[4,32,512]{2,1,0:T(8,128)(2,1)S(1)} %constant_dynamic-update-slice_fusion.refs_0_), channel_id=1, source_target_pairs={{0,4},{4,0},{8,12},{12,8},{16,20},{20,16},{24,28},{28,24},{1,5},{5... | collective-permute-start | bytes 393224 | tf_op jit(solution)/shard_map/ppermute | solution.py:19
  48.4 16.2 %collective-permute-start.20 = (bf16[2,160,512]{2,1,0:T(8,128)(2,1)S(1)}, bf16[2,160,512]{2,1,0:T(8,128)(2,1)S(1)}, u32[]{:S(2)}, u32[]{:S(2)}) collective-permute-start(bf16[2,160,512]{2,1,0:T(8,128)(2,1)S(1)} %get-tuple-element.24), channel_id=1, source_target_pairs={{0,1},{1,0},{2,3},{3,2},{4,5},{5,4},{6,7},{7,6},{8,9},{9,8},{10,11... | collective-permute-start | bytes 983048 | tf_op jit(solution)/shard_map/ppermute | solution.py:19
  49.6 14.8 %collective-permute-start.6 = (bf16[288,512]{1,0:T(8,128)(2,1)S(1)}, bf16[288,512]{1,0:T(8,128)(2,1)S(1)}, u32[]{:S(2)}, u32[]{:S(2)}) collective-permute-start(bf16[288,512]{1,0:T(8,128)(2,1)S(1)} %shard_map.76.refs_0_), channel_id=1, source_target_pairs={{0,4},{4,0},{8,12},{12,8},{16,20},{20,16},{24,28},{28,24},{1,5},{5... | collective-permute-start | bytes 884744 | tf_op jit(solution)/shard_map/ppermute | solution.py:19
  52.0 12.4 %collective-permute-start.7 = (bf16[256,512]{1,0:T(8,128)(2,1)S(1)}, bf16[256,512]{1,0:T(8,128)(2,1)S(1)}, u32[]{:S(2)}, u32[]{:S(2)}) collective-permute-start(bf16[256,512]{1,0:T(8,128)(2,1)S(1)} %get-tuple-element.19), channel_id=1, source_target_pairs={{0,4},{4,0},{8,12},{12,8},{16,20},{20,16},{24,28},{28,24},{1,5},{5... | collective-permute-start | bytes 786440 | tf_op jit(solution)/shard_map/ppermute | solution.py:19
  52.0 23.3 %collective-permute-start.10 = (bf16[544,512]{1,0:T(8,128)(2,1)S(1)}, bf16[544,512]{1,0:T(8,128)(2,1)S(1)}, u32[]{:S(2)}, u32[]{:S(2)}) collective-permute-start(bf16[544,512]{1,0:T(8,128)(2,1)S(1)} %get-tuple-element.18.whole), channel_id=1, source_target_pairs={{0,1},{1,0},{2,3},{3,2},{4,5},{5,4},{6,7},{7,6},{8,9},{9,8},{10,11... | collective-permute-start | bytes 1671176 | tf_op jit(solution)/shard_map/ppermute | solution.py:19
  52.1 23.2 %collective-permute-start.11 = (bf16[544,512]{1,0:T(8,128)(2,1)S(1)}, bf16[544,512]{1,0:T(8,128)(2,1)S(1)}, u32[]{:S(2)}, u32[]{:S(2)}) collective-permute-start(bf16[544,512]{1,0:T(8,128)(2,1)S(1)} %get-tuple-element.18.whole), channel_id=1, source_target_pairs={{0,3},{1,2},{2,1},{3,0},{4,7},{5,6},{6,5},{7,4},{8,11},{9,10},{10,... | collective-permute-start | bytes 1671176 | tf_op jit(solution)/shard_map/ppermute | solution.py:19
  64.3 11.0 %collective-permute-start.9 = (bf16[256,512]{1,0:T(8,128)(2,1)S(1)}, bf16[256,512]{1,0:T(8,128)(2,1)S(1)}, u32[]{:S(2)}, u32[]{:S(2)}) collective-permute-start(bf16[256,512]{1,0:T(8,128)(2,1)S(1)} %collective-permute-done.7.refs_1_), channel_id=1, source_target_pairs={{0,8},{4,28},{8,16},{12,4},{16,24},{20,12},{24,0},{28,20},{1,9},{5... | collective-permute-start | bytes 786440 | tf_op jit(solution)/shard_map/ppermute | solution.py:19
  64.4 15.7 %collective-permute-start.8 = (bf16[288,512]{1,0:T(8,128)(2,1)S(1)}, bf16[288,512]{1,0:T(8,128)(2,1)S(1)}, u32[]{:S(2)}, u32[]{:S(2)}) collective-permute-start(bf16[288,512]{1,0:T(8,128)(2,1)S(1)} %collective-permute-done.6.refs_0_), channel_id=1, source_target_pairs={{0,8},{4,28},{8,16},{12,4},{16,24},{20,12},{24,0},{28,20},{1,9},{5... | collective-permute-start | bytes 884744 | tf_op jit(solution)/shard_map/ppermute | solution.py:19
  64.7 16.3 %collective-permute-start.21 = (bf16[160,512]{1,0:T(8,128)(2,1)S(1)}, bf16[160,512]{1,0:T(8,128)(2,1)S(1)}, u32[]{:S(2)}, u32[]{:S(2)}) collective-permute-start(bf16[160,512]{1,0:T(8,128)(2,1)S(1)} %fusion), channel_id=1, source_target_pairs={{0,2},{1,3},{2,0},{3,1},{4,6},{5,7},{6,4},{7,5},{8,10},{9,11},{10,... | collective-permute-start | bytes 491528 | tf_op jit(solution)/shard_map/ppermute | solution.py:19
  (5 other events, 11.5 us)
